TPU v7x, 256 devices: a 4x2x16 block of a 4x16x16 slice. The times are simulated.
256 devices in a mesh: cand: 2 (over y), gx: 64 (over x, z), gy: 2 (over core).
Axes of the slice: x: 4, y: 2, z: 16, core: 2. Of those that a mesh axis runs over, the one named last changes fastest.
The devices are a block of a 4x16x16 slice.
Arguments:
- electric: float32 [2, 3, 512, 64, 128], P(None, None, ('cand', 'gx'), 'gy'), parts along dimension 2, may hold values from -6 to 6
- magnetic: float32 [2, 3, 512, 64, 128], P(None, None, ('cand', 'gx'), 'gy'), parts along dimension 2, may hold values from -6 to 6
- density: float32 [512, 64, 128], P(('cand', 'gx'), 'gy'), parts along dimension 0, may hold values from 0 to 0.1
- design_mask: int32 [512, 64, 128], P(('cand', 'gx'), 'gy'), parts along dimension 0, may hold values 0 or 1
- planes: int32 [4], P('cand'), parts along dimension 0, may hold values from 8 to 119
- profiles: float32 [2, 512, 64], P(None, ('cand', 'gx'), 'gy'), parts along dimension 1, may hold values from -6 to 6
- waveforms: float32 [2, 16], P(None, 'cand'), parts along dimension 1, may hold values from -4 to 4
Outputs:
- electric_out: float32 [2, 3, 512, 64, 128], P(None, None, ('cand', 'gx'), 'gy'), parts along dimension 2
- magnetic_out: float32 [2, 3, 512, 64, 128], P(None, None, ('cand', 'gx'), 'gy'), parts along dimension 2
- gradient: float32 [512, 64, 128], P(('cand', 'gx'), 'gy'), parts along dimension 0
There are 2 independent parts, one for each index of `cand`. A program takes and returns all parts, laid end to end along the dimension named above; each array names one. Nothing has to cross between parts.
All inputs are finite; a program needn't handle non-finite values. No bound on the sum of `design_mask` on one device may be relied on, other than what follows from the above.
Results may differ from a plain program's by a relative error of at most 0.00016.
Values sent between devices are 32-bit elements; how exact they have to be, the bound alone decides.
A program may use at most 64 MiB of HBM per device.

v0:
```python
import jax
import jax.numpy as jnp
from jax import lax
from jax.sharding import Mesh
from jax.sharding import PartitionSpec as P

STEPS = 8
PMLW = 8
GX = ("gx_0", "gx_1")
GX_GY = ("gx_0", "gx_1", "gy")
CAND_GX = ("cand", "gx_0", "gx_1")


step_dt = 0.7
contrast = 5.0
sigma_max = 2.0
small_eps = 1e-06
inv_spacing = 0.5


def with_halo(block, sides, width):
    for axis, dim in sides:
        count = lax.axis_size(axis)
        forward = [(i, i + 1) for i in range(count - 1)]
        backward = [(target, source) for source, target in forward]
        low = lax.ppermute(
            lax.slice_in_dim(block, block.shape[dim] - width, None, axis=dim), axis, forward
        )
        high = lax.ppermute(lax.slice_in_dim(block, 0, width, axis=dim), axis, backward)
        block = jnp.concatenate([low, block, high], axis=dim)
    return block


def over_axes(x, axes):
    for axis in axes:
        x = lax.psum(x, axis)
    return x


def coefficients(depth_cells, layer):
    zpos = jnp.arange(depth_cells).astype(jnp.float32)
    lower = (layer - zpos - 0.5) / layer
    upper = (zpos + 0.5 - (depth_cells - layer)) / layer
    depth = jnp.maximum(jnp.maximum(lower, upper), 0.0)
    sigma = sigma_max * depth * depth * depth
    half = sigma * step_dt / 2.0
    return ((1.0 - half) / (1.0 + half), step_dt / (1.0 + half))


def fwd_diff(field, upper, axis):
    rest = lax.slice_in_dim(field, 1, field.shape[axis], axis=axis)
    return jnp.concatenate([rest, upper], axis) - field


def bwd_diff(field, lower, axis):
    rest = lax.slice_in_dim(field, 0, field.shape[axis] - 1, axis=axis)
    return field - jnp.concatenate([lower, rest], axis)


def fwd_z(field):
    return (
        jnp.concatenate([field[..., 1:], jnp.zeros_like(field[..., :1])], -1) - field
    ) * inv_spacing


def bwd_z(field):
    return (
        field - jnp.concatenate([jnp.zeros_like(field[..., :1]), field[..., :-1]], -1)
    ) * inv_spacing


def magnetic_update(elec, magn, x_upper, y_upper, decay, gain):
    ex, ey, ez = (elec[:, 0], elec[:, 1], elec[:, 2])
    curl_x = fwd_diff(ez, y_upper[:, 1], 2) * inv_spacing - fwd_z(ey)
    curl_y = fwd_z(ex) - fwd_diff(ez, x_upper[:, 1], 1)
    curl_z = fwd_diff(ey, x_upper[:, 0], 1) - fwd_diff(ex, y_upper[:, 0], 2) * inv_spacing
    curl = jnp.stack([curl_x, curl_y, curl_z], 1)
    return decay * magn - gain * curl


def electric_update(elec, magn, x_lower, y_lower, decay, gain, inv_eps, drive):
    hx, hy, hz = (magn[:, 0], magn[:, 1], magn[:, 2])
    curl_x = bwd_diff(hz, y_lower[:, 1], 2) * inv_spacing - bwd_z(hy)
    curl_y = bwd_z(hx) - bwd_diff(hz, x_lower[:, 1], 1)
    curl_z = bwd_diff(hy, x_lower[:, 0], 1) - bwd_diff(hx, y_lower[:, 0], 2) * inv_spacing
    new_x = decay * elec[:, 0] + gain * (inv_eps * curl_x - drive)
    new_y = decay * elec[:, 1] + gain * (inv_eps * curl_y)
    new_z = decay * elec[:, 2] + gain * (inv_eps * curl_z)
    return jnp.stack([new_x, new_y, new_z], 1)


def correlate(elec):
    return jnp.sum(elec[0] * elec[1], axis=0)


def inside_mask(count, start, total):
    where = start + jnp.arange(count)
    return ((where >= 0) & (where < total)).astype(jnp.float32)


def shards(electric, magnetic, density, design_mask, planes, profiles, waveforms):
    sets, comps, width_x, width_y, depth_z = electric.shape
    decay, gain = coefficients(depth_z, PMLW)
    flags = design_mask.astype(jnp.float32)
    inv_eps = 1.0 / (1.0 + contrast * density * flags)
    zidx = jnp.arange(depth_z)
    source = profiles[0][:, :, None] * (zidx == planes[0]).astype(jnp.float32)
    adjoint = profiles[1][:, :, None] * (zidx == planes[1]).astype(jnp.float32)
    probe = (zidx == planes[1]).astype(jnp.float32)
    total_x = width_x * lax.axis_size(GX)
    total_y = width_y * lax.axis_size("gy")
    elec, magn = (electric, magnetic)
    corr = jnp.zeros((width_x, width_y, depth_z), jnp.float32)
    rim = 2
    inv_wide, source_wide, adjoint_wide = (
        with_halo(inv_eps, ((GX, 0), ("gy", 1)), rim),
        with_halo(source, ((GX, 0), ("gy", 1)), rim),
        with_halo(adjoint, ((GX, 0), ("gy", 1)), rim),
    )
    valid_x = inside_mask(width_x + 2 * rim, lax.axis_index(GX) * width_x - rim, total_x)
    valid_y = inside_mask(width_y + 2 * rim, lax.axis_index("gy") * width_y - rim, total_y)
    valid = valid_x[:, None, None] * valid_y[None, :, None]
    x_zero = jnp.zeros((sets, 2, 1, width_y + 2 * rim, depth_z), jnp.float32)
    y_zero = jnp.zeros((sets, 2, width_x + 2 * rim, 1, depth_z), jnp.float32)
    for rounds in range(STEPS // rim):
        elec_wide, magn_wide = (
            with_halo(elec, ((GX, 2), ("gy", 3)), rim),
            with_halo(magn, ((GX, 2), ("gy", 3)), rim),
        )
        for inner_step in range(rim):
            step = rounds * rim + inner_step
            magn_wide = magnetic_update(elec_wide, magn_wide, x_zero, y_zero, decay, gain) * valid
            drive = jnp.stack([source_wide * waveforms[0, step], adjoint_wide * waveforms[1, step]])
            elec_wide = (
                electric_update(elec_wide, magn_wide, x_zero, y_zero, decay, gain, inv_wide, drive)
                * valid
            )
            corr = corr + correlate(elec_wide[:, :, rim : rim + width_x, rim : rim + width_y])
        elec = elec_wide[:, :, rim : rim + width_x, rim : rim + width_y]
        magn = magn_wide[:, :, rim : rim + width_x, rim : rim + width_y]
    local_power = jnp.sum(elec[0] * elec[0] * probe)
    power = over_axes(local_power, GX_GY) / (total_x * total_y)
    gradient = flags * contrast * inv_eps * inv_eps * step_dt * corr / (power + small_eps)
    return (elec, magn, gradient)


def solution(mesh):
    finer = Mesh(
        mesh.devices.reshape(mesh.shape["cand"], 4, 16, mesh.shape["gy"]),
        ("cand", "gx_0", "gx_1", "gy"),
    )
    return jax.shard_map(
        shards,
        mesh=finer,
        in_specs=(
            P(None, None, CAND_GX, "gy", None),
            P(None, None, CAND_GX, "gy", None),
            P(CAND_GX, "gy", None),
            P(CAND_GX, "gy", None),
            P("cand"),
            P(None, CAND_GX, "gy"),
            P(None, "cand"),
        ),
        out_specs=(
            P(None, None, CAND_GX, "gy", None),
            P(None, None, CAND_GX, "gy", None),
            P(CAND_GX, "gy", None),
        ),
        check_vma=False,
    )
```

profile of v0, /device:TPU:40, one launch (start us, length us, event | category | flops | bytes accessed | tf_op | source)
XLA Modules:
  0.0 232.8 jit_solution(4798826788056224946)
XLA Ops:
  1.7 4.7 %collective-permute-start.4 = (f32[2,32,128]{2,0,1:T(2,128)S(1)}, f32[2,32,128]{2,0,1:T(2,128)S(1)}, u32[]{:S(2)}, u32[]{:S(2)}) collective-permute-start(f32[2,32,128]{2,0,1:T(2,128)S(1)} %get-tuple-element.162), channel_id=1, source_target_pairs={{0,2},{2,4},{4,6},{6,8},{8,10},{10,12},{12,14},{14,16},{16,18},{18... | collective-permute-start | bytes 98312 | tf_op jit(solution)/shard_map/ppermute | solution.py:26
  10.6 5.4 %collective-permute-start.16 = (f32[2,32,128]{2,0,1:T(2,128)S(1)}, f32[2,32,128]{2,0,1:T(2,128)S(1)}, u32[]{:S(2)}, u32[]{:S(2)}) collective-permute-start(f32[2,32,128]{2,0,1:T(2,128)S(1)} %get-tuple-element.160), channel_id=1, source_target_pairs={{0,2},{2,4},{4,6},{6,8},{8,10},{10,12},{12,14},{14,16},{16,18},{18... | collective-permute-start | bytes 98312 | tf_op jit(solution)/shard_map/ppermute | solution.py:26
  16.9 4.7 %collective-permute-start.12 = (f32[2,32,128]{2,0,1:T(2,128)S(1)}, f32[2,32,128]{2,0,1:T(2,128)S(1)}, u32[]{:S(2)}, u32[]{:S(2)}) collective-permute-start(f32[2,32,128]{2,0,1:T(2,128)S(1)} %get-tuple-element.158), channel_id=1, source_target_pairs={{0,2},{2,4},{4,6},{6,8},{8,10},{10,12},{12,14},{14,16},{16,18},{18... | collective-permute-start | bytes 98312 | tf_op jit(solution)/shard_map/ppermute | solution.py:26
  29.4 5.2 %collective-permute-start.8 = (f32[2,3,2,32,128]{4,2,3,0,1:T(2,128)S(1)}, f32[2,3,2,32,128]{4,2,3,0,1:T(2,128)S(1)}, u32[]{:S(2)}, u32[]{:S(2)}) collective-permute-start(f32[2,3,2,32,128]{4,2,3,0,1:T(2,128)S(1)} %get-tuple-element.130), channel_id=1, source_target_pairs={{0,2},{2,4},{4,6},{6,8},{8,10},{10,12},{12,14},{14,16},{16,18},{18... | collective-permute-start | bytes 589832 | tf_op jit(solution)/shard_map/ppermute | solution.py:26
  34.7 5.2 %collective-permute-start = (f32[2,3,2,32,128]{4,2,3,0,1:T(2,128)S(1)}, f32[2,3,2,32,128]{4,2,3,0,1:T(2,128)S(1)}, u32[]{:S(2)}, u32[]{:S(2)}) collective-permute-start(f32[2,3,2,32,128]{4,2,3,0,1:T(2,128)S(1)} %get-tuple-element.128), channel_id=1, source_target_pairs={{0,2},{2,4},{4,6},{6,8},{8,10},{10,12},{12,14},{14,16},{16,18},{18... | collective-permute-start | bytes 589832 | tf_op jit(solution)/shard_map/ppermute | solution.py:26
  43.9 3.1 %collective-permute-start.14 = (f32[8,2,128]{2,0,1:T(8,128)S(1)}, f32[8,2,128]{2,0,1:T(8,128)S(1)}, u32[]{:S(2)}, u32[]{:S(2)}) collective-permute-start(f32[8,2,128]{2,0,1:T(8,128)S(1)} %get-tuple-element.148), channel_id=1, source_target_pairs={{0,1},{2,3},{4,5},{6,7},{8,9},{10,11},{12,13},{14,15},{16,17},{18,... | collective-permute-start | bytes 24584 | tf_op jit(solution)/shard_map/ppermute | solution.py:26
  50.9 2.5 %broadcast_multiply_fusion.2 = (f32[1,8,36,128]{3,1,2,0:T(8,128)S(1)}, f32[1,8,36,128]{3,1,2,0:T(8,128)S(1)}, f32[1,8,36,128]{3,1,2,0:T(8,128)S(1)}, f32[1,8,36,128]{3,1,2,0:T(8,128)S(1)}) fusion(f32[]{:T(128)} %bitcast.103, f32[1,8,2,128]{3,1,2,0:T(8,128)S(1)} %bitcast.541, f32[1,8,32,128]{3,1,2,0:T(8,128)S(1)} %get-tuple-element.154, ...), kind=kLoop, calls=%fused_computation.186 | loop fusion | flops 221184 | bytes 737296 | tf_op jit(solution)/shard_map/mul | solution.py:133
  53.4 3.1 %collective-permute-start.6 = (f32[8,2,128]{2,0,1:T(8,128)S(1)}, f32[8,2,128]{2,0,1:T(8,128)S(1)}, u32[]{:S(2)}, u32[]{:S(2)}) collective-permute-start(f32[8,2,128]{2,0,1:T(8,128)S(1)} %get-tuple-element.156), channel_id=1, source_target_pairs={{0,1},{2,3},{4,5},{6,7},{8,9},{10,11},{12,13},{14,15},{16,17},{18,... | collective-permute-start | bytes 24584 | tf_op jit(solution)/shard_map/ppermute | solution.py:26
  57.8 2.6 %broadcast_multiply_fusion.1 = (f32[1,8,36,128]{3,1,2,0:T(8,128)S(1)}, f32[1,8,36,128]{3,1,2,0:T(8,128)S(1)}, f32[1,8,36,128]{3,1,2,0:T(8,128)S(1)}, f32[1,8,36,128]{3,1,2,0:T(8,128)S(1)}) fusion(f32[]{:T(128)} %bitcast.116, f32[1,8,2,128]{3,1,2,0:T(8,128)S(1)} %bitcast.536, f32[1,8,32,128]{3,1,2,0:T(8,128)S(1)} %get-tuple-element.150, ...), kind=kLoop, calls=%fused_computation.185 | loop fusion | flops 221184 | bytes 737296 | tf_op jit(solution)/shard_map/mul | solution.py:133
  60.4 2.6 %broadcast_multiply_fusion.3 = (f32[1,8,36,128]{3,1,2,0:T(8,128)S(1)}, f32[1,8,36,128]{3,1,2,0:T(8,128)S(1)}, f32[1,8,36,128]{3,1,2,0:T(8,128)S(1)}, f32[1,8,36,128]{3,1,2,0:T(8,128)S(1)}) fusion(f32[]{:T(128)} %bitcast.102, f32[1,8,2,128]{3,1,2,0:T(8,128)S(1)} %bitcast.537, f32[1,8,32,128]{3,1,2,0:T(8,128)S(1)} %get-tuple-element.150, ...), kind=kLoop, calls=%fused_computation.187 | loop fusion | flops 221184 | bytes 737296 | tf_op jit(solution)/shard_map/mul | solution.py:133
  64.5 3.1 %collective-permute-start.2 = (f32[2,3,8,2,128]{4,2,3,0,1:T(8,128)S(1)}, f32[2,3,8,2,128]{4,2,3,0,1:T(8,128)S(1)}, u32[]{:S(2)}, u32[]{:S(2)}) collective-permute-start(f32[2,3,8,2,128]{4,2,3,0,1:T(8,128)S(1)} %get-tuple-element.124), channel_id=1, source_target_pairs={{0,1},{2,3},{4,5},{6,7},{8,9},{10,11},{12,13},{14,15},{16,17},{18,... | collective-permute-start | bytes 147464 | tf_op jit(solution)/shard_map/ppermute | solution.py:26
  68.9 4.3 %collective-permute-done.9 = f32[2,3,2,32,128]{4,2,3,0,1:T(2,128)S(1)} collective-permute-done((f32[2,3,2,32,128]{4,2,3,0,1:T(2,128)S(1)}, f32[2,3,2,32,128]{4,2,3,0,1:T(2,128)S(1)}, u32[]{:S(2)}, u32[]{:S(2)}) %collective-permute-start.9) | collective-permute-done | bytes 196640 | tf_op jit(solution)/shard_map/ppermute | solution.py:29
  81.7 5.5 %collective-permute-start.20 = (f32[2,3,2,32,128]{4,2,3,0,1:T(2,128)S(1)}, f32[2,3,2,32,128]{4,2,3,0,1:T(2,128)S(1)}, u32[]{:S(2)}, u32[]{:S(2)}) collective-permute-start(f32[2,3,2,32,128]{4,2,3,0,1:T(2,128)S(1)} %get-tuple-element.90), channel_id=1, source_target_pairs={{0,2},{2,4},{4,6},{6,8},{8,10},{10,12},{12,14},{14,16},{16,18},{18... | collective-permute-start | bytes 589832 | tf_op jit(solution)/shard_map/ppermute | solution.py:26
  88.8 5.8 %collective-permute-start.24 = (f32[2,3,2,32,128]{4,2,3,0,1:T(2,128)S(1)}, f32[2,3,2,32,128]{4,2,3,0,1:T(2,128)S(1)}, u32[]{:S(2)}, u32[]{:S(2)}) collective-permute-start(f32[2,3,2,32,128]{4,2,3,0,1:T(2,128)S(1)} %get-tuple-element.95), channel_id=1, source_target_pairs={{0,2},{2,4},{4,6},{6,8},{8,10},{10,12},{12,14},{14,16},{16,18},{18... | collective-permute-start | bytes 589832 | tf_op jit(solution)/shard_map/ppermute | solution.py:26
  100.2 4.4 %collective-permute-done.25 = f32[2,3,2,32,128]{4,2,3,0,1:T(2,128)S(1)} collective-permute-done((f32[2,3,2,32,128]{4,2,3,0,1:T(2,128)S(1)}, f32[2,3,2,32,128]{4,2,3,0,1:T(2,128)S(1)}, u32[]{:S(2)}, u32[]{:S(2)}) %collective-permute-start.25) | collective-permute-done | bytes 196640 | tf_op jit(solution)/shard_map/ppermute | solution.py:29
  112.2 4.0 %collective-permute-start.28 = (f32[2,3,2,32,128]{4,2,3,0,1:T(2,128)S(1)}, f32[2,3,2,32,128]{4,2,3,0,1:T(2,128)S(1)}, u32[]{:S(2)}, u32[]{:S(2)}) collective-permute-start(f32[2,3,2,32,128]{4,2,3,0,1:T(2,128)S(1)} %get-tuple-element.68), channel_id=1, source_target_pairs={{0,2},{2,4},{4,6},{6,8},{8,10},{10,12},{12,14},{14,16},{16,18},{18... | collective-permute-start | bytes 589832 | tf_op jit(solution)/shard_map/ppermute | solution.py:26
  117.8 5.8 %collective-permute-start.32 = (f32[2,3,2,32,128]{4,2,3,0,1:T(2,128)S(1)}, f32[2,3,2,32,128]{4,2,3,0,1:T(2,128)S(1)}, u32[]{:S(2)}, u32[]{:S(2)}) collective-permute-start(f32[2,3,2,32,128]{4,2,3,0,1:T(2,128)S(1)} %get-tuple-element.73), channel_id=1, source_target_pairs={{0,2},{2,4},{4,6},{6,8},{8,10},{10,12},{12,14},{14,16},{16,18},{18... | collective-permute-start | bytes 589832 | tf_op jit(solution)/shard_map/ppermute | solution.py:26
  129.5 3.9 %collective-permute-done.33 = f32[2,3,2,32,128]{4,2,3,0,1:T(2,128)S(1)} collective-permute-done((f32[2,3,2,32,128]{4,2,3,0,1:T(2,128)S(1)}, f32[2,3,2,32,128]{4,2,3,0,1:T(2,128)S(1)}, u32[]{:S(2)}, u32[]{:S(2)}) %collective-permute-start.33) | collective-permute-done | bytes 196640 | tf_op jit(solution)/shard_map/ppermute | solution.py:29
  141.1 4.4 %collective-permute-start.36 = (f32[2,3,2,32,128]{4,2,3,0,1:T(2,128)S(1)}, f32[2,3,2,32,128]{4,2,3,0,1:T(2,128)S(1)}, u32[]{:S(2)}, u32[]{:S(2)}) collective-permute-start(f32[2,3,2,32,128]{4,2,3,0,1:T(2,128)S(1)} %get-tuple-element.46), channel_id=1, source_target_pairs={{0,2},{2,4},{4,6},{6,8},{8,10},{10,12},{12,14},{14,16},{16,18},{18... | collective-permute-start | bytes 589832 | tf_op jit(solution)/shard_map/ppermute | solution.py:26
  147.0 5.5 %collective-permute-start.40 = (f32[2,3,2,32,128]{4,2,3,0,1:T(2,128)S(1)}, f32[2,3,2,32,128]{4,2,3,0,1:T(2,128)S(1)}, u32[]{:S(2)}, u32[]{:S(2)}) collective-permute-start(f32[2,3,2,32,128]{4,2,3,0,1:T(2,128)S(1)} %get-tuple-element.51), channel_id=1, source_target_pairs={{0,2},{2,4},{4,6},{6,8},{8,10},{10,12},{12,14},{14,16},{16,18},{18... | collective-permute-start | bytes 589832 | tf_op jit(solution)/shard_map/ppermute | solution.py:26
  158.1 4.1 %collective-permute-done.41 = f32[2,3,2,32,128]{4,2,3,0,1:T(2,128)S(1)} collective-permute-done((f32[2,3,2,32,128]{4,2,3,0,1:T(2,128)S(1)}, f32[2,3,2,32,128]{4,2,3,0,1:T(2,128)S(1)}, u32[]{:S(2)}, u32[]{:S(2)}) %collective-permute-start.41) | collective-permute-done | bytes 196640 | tf_op jit(solution)/shard_map/ppermute | solution.py:29
  170.5 26.2 %psum.21 = f32[]{:T(128)} all-reduce(f32[]{:T(128)} %fusion.47), channel_id=1, replica_groups=mesh['cand'=2,'gx_0'=4,'gx_1'=16,'gy'=2] {'gx_0'}, use_global_device_ids=true, to_apply=%region_9.0 | all-reduce | flops 1 | bytes 8 | tf_op jit(solution)/shard_map/psum | solution.py:36
  196.8 29.8 %psum.22 = f32[]{:T(128)} all-reduce(f32[]{:T(128)} %psum.21), channel_id=1, replica_groups=mesh['cand'=2,'gx_0'=4,'gx_1'=16,'gy'=2] {'gx_1'}, use_global_device_ids=true, to_apply=%region_10.0 | all-reduce | flops 1 | bytes 8 | tf_op jit(solution)/shard_map/psum | solution.py:36
  227.4 3.1 %psum.23 = f32[]{:T(128)} all-reduce(f32[]{:T(128)} %psum.22), channel_id=1, replica_groups=mesh['cand'=2,'gx_0'=4,'gx_1'=16,'gy'=2] {'gy'}, use_global_device_ids=true, to_apply=%region_11.0 | all-reduce | flops 1 | bytes 8 | tf_op jit(solution)/shard_map/psum | solution.py:36
  (267 shorter events, 80.8 us)
Async XLA Ops:
  1.7 39.6 %collective-permute-start.4 = (f32[2,32,128]{2,0,1:T(2,128)S(1)}, f32[2,32,128]{2,0,1:T(2,128)S(1)}, u32[]{:S(2)}, u32[]{:S(2)}) collective-permute-start(f32[2,32,128]{2,0,1:T(2,128)S(1)} %get-tuple-element.162), channel_id=1, source_target_pairs={{0,2},{2,4},{4,6},{6,8},{8,10},{10,12},{12,14},{14,16},{16,18},{18... | collective-permute-start | bytes 98312 | tf_op jit(solution)/shard_map/ppermute | solution.py:26
  6.4 36.2 %collective-permute-start.5 = (f32[2,32,128]{2,0,1:T(2,128)S(1)}, f32[2,32,128]{2,0,1:T(2,128)S(1)}, u32[]{:S(2)}, u32[]{:S(2)}) collective-permute-start(f32[2,32,128]{2,0,1:T(2,128)S(1)} %get-tuple-element.163), channel_id=1, source_target_pairs={{2,0},{4,2},{6,4},{8,6},{10,8},{12,10},{14,12},{16,14},{18,16},{20... | collective-permute-start | bytes 98312 | tf_op jit(solution)/shard_map/ppermute | solution.py:29
  10.6 24.0 %collective-permute-start.16 = (f32[2,32,128]{2,0,1:T(2,128)S(1)}, f32[2,32,128]{2,0,1:T(2,128)S(1)}, u32[]{:S(2)}, u32[]{:S(2)}) collective-permute-start(f32[2,32,128]{2,0,1:T(2,128)S(1)} %get-tuple-element.160), channel_id=1, source_target_pairs={{0,2},{2,4},{4,6},{6,8},{8,10},{10,12},{12,14},{14,16},{16,18},{18... | collective-permute-start | bytes 98312 | tf_op jit(solution)/shard_map/ppermute | solution.py:26
  26.0 13.8 %collective-permute-start.17 = (f32[2,32,128]{2,0,1:T(2,128)S(1)}, f32[2,32,128]{2,0,1:T(2,128)S(1)}, u32[]{:S(2)}, u32[]{:S(2)}) collective-permute-start(f32[2,32,128]{2,0,1:T(2,128)S(1)} %get-tuple-element.161), channel_id=1, source_target_pairs={{2,0},{4,2},{6,4},{8,6},{10,8},{12,10},{14,12},{16,14},{18,16},{20... | collective-permute-start | bytes 98312 | tf_op jit(solution)/shard_map/ppermute | solution.py:29
  29.4 39.4 %collective-permute-start.8 = (f32[2,3,2,32,128]{4,2,3,0,1:T(2,128)S(1)}, f32[2,3,2,32,128]{4,2,3,0,1:T(2,128)S(1)}, u32[]{:S(2)}, u32[]{:S(2)}) collective-permute-start(f32[2,3,2,32,128]{4,2,3,0,1:T(2,128)S(1)} %get-tuple-element.130), channel_id=1, source_target_pairs={{0,2},{2,4},{4,6},{6,8},{8,10},{10,12},{12,14},{14,16},{16,18},{18... | collective-permute-start | bytes 589832 | tf_op jit(solution)/shard_map/ppermute | solution.py:26
  34.7 29.7 %collective-permute-start = (f32[2,3,2,32,128]{4,2,3,0,1:T(2,128)S(1)}, f32[2,3,2,32,128]{4,2,3,0,1:T(2,128)S(1)}, u32[]{:S(2)}, u32[]{:S(2)}) collective-permute-start(f32[2,3,2,32,128]{4,2,3,0,1:T(2,128)S(1)} %get-tuple-element.128), channel_id=1, source_target_pairs={{0,2},{2,4},{4,6},{6,8},{8,10},{10,12},{12,14},{14,16},{16,18},{18... | collective-permute-start | bytes 589832 | tf_op jit(solution)/shard_map/ppermute | solution.py:26
  39.9 24.5 %collective-permute-start.1 = (f32[2,3,2,32,128]{4,2,3,0,1:T(2,128)S(1)}, f32[2,3,2,32,128]{4,2,3,0,1:T(2,128)S(1)}, u32[]{:S(2)}, u32[]{:S(2)}) collective-permute-start(f32[2,3,2,32,128]{4,2,3,0,1:T(2,128)S(1)} %get-tuple-element.129), channel_id=1, source_target_pairs={{2,0},{4,2},{6,4},{8,6},{10,8},{12,10},{14,12},{16,14},{18,16},{20... | collective-permute-start | bytes 589832 | tf_op jit(solution)/shard_map/ppermute | solution.py:29
  53.4 9.6 %collective-permute-start.6 = (f32[8,2,128]{2,0,1:T(8,128)S(1)}, f32[8,2,128]{2,0,1:T(8,128)S(1)}, u32[]{:S(2)}, u32[]{:S(2)}) collective-permute-start(f32[8,2,128]{2,0,1:T(8,128)S(1)} %get-tuple-element.156), channel_id=1, source_target_pairs={{0,1},{2,3},{4,5},{6,7},{8,9},{10,11},{12,13},{14,15},{16,17},{18,... | collective-permute-start | bytes 24584 | tf_op jit(solution)/shard_map/ppermute | solution.py:26
  63.0 10.2 %collective-permute-start.9 = (f32[2,3,2,32,128]{4,2,3,0,1:T(2,128)S(1)}, f32[2,3,2,32,128]{4,2,3,0,1:T(2,128)S(1)}, u32[]{:S(2)}, u32[]{:S(2)}) collective-permute-start(f32[2,3,2,32,128]{4,2,3,0,1:T(2,128)S(1)} %get-tuple-element.131), channel_id=1, source_target_pairs={{2,0},{4,2},{6,4},{8,6},{10,8},{12,10},{14,12},{16,14},{18,16},{20... | collective-permute-start | bytes 589832 | tf_op jit(solution)/shard_map/ppermute | solution.py:29
  64.5 12.3 %collective-permute-start.2 = (f32[2,3,8,2,128]{4,2,3,0,1:T(8,128)S(1)}, f32[2,3,8,2,128]{4,2,3,0,1:T(8,128)S(1)}, u32[]{:S(2)}, u32[]{:S(2)}) collective-permute-start(f32[2,3,8,2,128]{4,2,3,0,1:T(8,128)S(1)} %get-tuple-element.124), channel_id=1, source_target_pairs={{0,1},{2,3},{4,5},{6,7},{8,9},{10,11},{12,13},{14,15},{16,17},{18,... | collective-permute-start | bytes 147464 | tf_op jit(solution)/shard_map/ppermute | solution.py:26
  81.7 14.3 %collective-permute-start.20 = (f32[2,3,2,32,128]{4,2,3,0,1:T(2,128)S(1)}, f32[2,3,2,32,128]{4,2,3,0,1:T(2,128)S(1)}, u32[]{:S(2)}, u32[]{:S(2)}) collective-permute-start(f32[2,3,2,32,128]{4,2,3,0,1:T(2,128)S(1)} %get-tuple-element.90), channel_id=1, source_target_pairs={{0,2},{2,4},{4,6},{6,8},{8,10},{10,12},{12,14},{14,16},{16,18},{18... | collective-permute-start | bytes 589832 | tf_op jit(solution)/shard_map/ppermute | solution.py:26
  87.2 10.2 %collective-permute-start.21 = (f32[2,3,2,32,128]{4,2,3,0,1:T(2,128)S(1)}, f32[2,3,2,32,128]{4,2,3,0,1:T(2,128)S(1)}, u32[]{:S(2)}, u32[]{:S(2)}) collective-permute-start(f32[2,3,2,32,128]{4,2,3,0,1:T(2,128)S(1)} %get-tuple-element.91), channel_id=1, source_target_pairs={{2,0},{4,2},{6,4},{8,6},{10,8},{12,10},{14,12},{16,14},{18,16},{20... | collective-permute-start | bytes 589832 | tf_op jit(solution)/shard_map/ppermute | solution.py:29
  88.8 11.4 %collective-permute-start.24 = (f32[2,3,2,32,128]{4,2,3,0,1:T(2,128)S(1)}, f32[2,3,2,32,128]{4,2,3,0,1:T(2,128)S(1)}, u32[]{:S(2)}, u32[]{:S(2)}) collective-permute-start(f32[2,3,2,32,128]{4,2,3,0,1:T(2,128)S(1)} %get-tuple-element.95), channel_id=1, source_target_pairs={{0,2},{2,4},{4,6},{6,8},{8,10},{10,12},{12,14},{14,16},{16,18},{18... | collective-permute-start | bytes 589832 | tf_op jit(solution)/shard_map/ppermute | solution.py:26
  94.7 9.9 %collective-permute-start.25 = (f32[2,3,2,32,128]{4,2,3,0,1:T(2,128)S(1)}, f32[2,3,2,32,128]{4,2,3,0,1:T(2,128)S(1)}, u32[]{:S(2)}, u32[]{:S(2)}) collective-permute-start(f32[2,3,2,32,128]{4,2,3,0,1:T(2,128)S(1)} %get-tuple-element.96), channel_id=1, source_target_pairs={{2,0},{4,2},{6,4},{8,6},{10,8},{12,10},{14,12},{16,14},{18,16},{20... | collective-permute-start | bytes 589832 | tf_op jit(solution)/shard_map/ppermute | solution.py:29
  97.5 10.0 %collective-permute-start.22 = (f32[2,3,8,2,128]{4,2,3,0,1:T(8,128)S(1)}, f32[2,3,8,2,128]{4,2,3,0,1:T(8,128)S(1)}, u32[]{:S(2)}, u32[]{:S(2)}) collective-permute-start(f32[2,3,8,2,128]{4,2,3,0,1:T(8,128)S(1)} %get-tuple-element.120), channel_id=1, source_target_pairs={{0,1},{2,3},{4,5},{6,7},{8,9},{10,11},{12,13},{14,15},{16,17},{18,... | collective-permute-start | bytes 147464 | tf_op jit(solution)/shard_map/ppermute | solution.py:26
  112.2 12.8 %collective-permute-start.28 = (f32[2,3,2,32,128]{4,2,3,0,1:T(2,128)S(1)}, f32[2,3,2,32,128]{4,2,3,0,1:T(2,128)S(1)}, u32[]{:S(2)}, u32[]{:S(2)}) collective-permute-start(f32[2,3,2,32,128]{4,2,3,0,1:T(2,128)S(1)} %get-tuple-element.68), channel_id=1, source_target_pairs={{0,2},{2,4},{4,6},{6,8},{8,10},{10,12},{12,14},{14,16},{16,18},{18... | collective-permute-start | bytes 589832 | tf_op jit(solution)/shard_map/ppermute | solution.py:26
  116.2 10.4 %collective-permute-start.29 = (f32[2,3,2,32,128]{4,2,3,0,1:T(2,128)S(1)}, f32[2,3,2,32,128]{4,2,3,0,1:T(2,128)S(1)}, u32[]{:S(2)}, u32[]{:S(2)}) collective-permute-start(f32[2,3,2,32,128]{4,2,3,0,1:T(2,128)S(1)} %get-tuple-element.69), channel_id=1, source_target_pairs={{2,0},{4,2},{6,4},{8,6},{10,8},{12,10},{14,12},{16,14},{18,16},{20... | collective-permute-start | bytes 589832 | tf_op jit(solution)/shard_map/ppermute | solution.py:29
  117.8 11.7 %collective-permute-start.32 = (f32[2,3,2,32,128]{4,2,3,0,1:T(2,128)S(1)}, f32[2,3,2,32,128]{4,2,3,0,1:T(2,128)S(1)}, u32[]{:S(2)}, u32[]{:S(2)}) collective-permute-start(f32[2,3,2,32,128]{4,2,3,0,1:T(2,128)S(1)} %get-tuple-element.73), channel_id=1, source_target_pairs={{0,2},{2,4},{4,6},{6,8},{8,10},{10,12},{12,14},{14,16},{16,18},{18... | collective-permute-start | bytes 589832 | tf_op jit(solution)/shard_map/ppermute | solution.py:26
  123.6 9.8 %collective-permute-start.33 = (f32[2,3,2,32,128]{4,2,3,0,1:T(2,128)S(1)}, f32[2,3,2,32,128]{4,2,3,0,1:T(2,128)S(1)}, u32[]{:S(2)}, u32[]{:S(2)}) collective-permute-start(f32[2,3,2,32,128]{4,2,3,0,1:T(2,128)S(1)} %get-tuple-element.74), channel_id=1, source_target_pairs={{2,0},{4,2},{6,4},{8,6},{10,8},{12,10},{14,12},{16,14},{18,16},{20... | collective-permute-start | bytes 589832 | tf_op jit(solution)/shard_map/ppermute | solution.py:29
  141.1 12.9 %collective-permute-start.36 = (f32[2,3,2,32,128]{4,2,3,0,1:T(2,128)S(1)}, f32[2,3,2,32,128]{4,2,3,0,1:T(2,128)S(1)}, u32[]{:S(2)}, u32[]{:S(2)}) collective-permute-start(f32[2,3,2,32,128]{4,2,3,0,1:T(2,128)S(1)} %get-tuple-element.46), channel_id=1, source_target_pairs={{0,2},{2,4},{4,6},{6,8},{8,10},{10,12},{12,14},{14,16},{16,18},{18... | collective-permute-start | bytes 589832 | tf_op jit(solution)/shard_map/ppermute | solution.py:26
  145.4 9.9 %collective-permute-start.37 = (f32[2,3,2,32,128]{4,2,3,0,1:T(2,128)S(1)}, f32[2,3,2,32,128]{4,2,3,0,1:T(2,128)S(1)}, u32[]{:S(2)}, u32[]{:S(2)}) collective-permute-start(f32[2,3,2,32,128]{4,2,3,0,1:T(2,128)S(1)} %get-tuple-element.47), channel_id=1, source_target_pairs={{2,0},{4,2},{6,4},{8,6},{10,8},{12,10},{14,12},{16,14},{18,16},{20... | collective-permute-start | bytes 589832 | tf_op jit(solution)/shard_map/ppermute | solution.py:29
  147.0 11.1 %collective-permute-start.40 = (f32[2,3,2,32,128]{4,2,3,0,1:T(2,128)S(1)}, f32[2,3,2,32,128]{4,2,3,0,1:T(2,128)S(1)}, u32[]{:S(2)}, u32[]{:S(2)}) collective-permute-start(f32[2,3,2,32,128]{4,2,3,0,1:T(2,128)S(1)} %get-tuple-element.51), channel_id=1, source_target_pairs={{0,2},{2,4},{4,6},{6,8},{8,10},{10,12},{12,14},{14,16},{16,18},{18... | collective-permute-start | bytes 589832 | tf_op jit(solution)/shard_map/ppermute | solution.py:26
  152.6 9.7 %collective-permute-start.41 = (f32[2,3,2,32,128]{4,2,3,0,1:T(2,128)S(1)}, f32[2,3,2,32,128]{4,2,3,0,1:T(2,128)S(1)}, u32[]{:S(2)}, u32[]{:S(2)}) collective-permute-start(f32[2,3,2,32,128]{4,2,3,0,1:T(2,128)S(1)} %get-tuple-element.52), channel_id=1, source_target_pairs={{2,0},{4,2},{6,4},{8,6},{10,8},{12,10},{14,12},{16,14},{18,16},{20... | collective-permute-start | bytes 589832 | tf_op jit(solution)/shard_map/ppermute | solution.py:29
  155.4 9.7 %collective-permute-start.38 = (f32[2,3,8,2,128]{4,2,3,0,1:T(8,128)S(1)}, f32[2,3,8,2,128]{4,2,3,0,1:T(8,128)S(1)}, u32[]{:S(2)}, u32[]{:S(2)}) collective-permute-start(f32[2,3,8,2,128]{4,2,3,0,1:T(8,128)S(1)} %get-tuple-element.112), channel_id=1, source_target_pairs={{0,1},{2,3},{4,5},{6,7},{8,9},{10,11},{12,13},{14,15},{16,17},{18,... | collective-permute-start | bytes 147464 | tf_op jit(solution)/shard_map/ppermute | solution.py:26
  (25 other events, 157.3 us)
where the time goes:
time: 235 us; the launch traced here: 233 us
  starting transfers between devices  106 us (45%)
  blocking collectives  59.1 us (25%)
  waiting for transfers between devices  26.3 us (11%)
  other arithmetic  24.8 us (11%)
  local copies, waits for them, and re-layouts  13.3 us (6%)
  between operations  3.09 us (1%)
    ppermute x22, starting transfers between devices, with_halo(): lax.ppermute(lax.slice_in_dim(block, block.shape[dim] - width, None, axis...  77 us
    psum x3, blocking collectives, over_axes(): x = lax.psum(x, axis)  59.1 us
    ppermute x22, starting transfers between devices, with_halo(): lax.ppermute(lax.slice_in_dim(block, 0, width, axis=dim), axis, backward)  29.2 us
    ppermute x22, waiting for transfers between devices, with_halo(): lax.ppermute(lax.slice_in_dim(block, 0, width, axis=dim), axis, backward)  26.2 us
    mul x2, other arithmetic, shards(): source_wide * waveforms[0, step]  5.2 us
    mul x2, other arithmetic, shards(): adjoint_wide * waveforms[1, step]  5.02 us
  transfers between devices with their start and end apart: 44, of which 12 were waited for; matrix products, arithmetic and copies ran while one was open for 9% of the time, Pallas kernels for 0%

commit v1 on v0

v1 whole, which is shorter than its diff:
```python
import jax
import jax.numpy as jnp
from jax import lax
from jax.experimental import pallas as pl
from jax.experimental.pallas import tpu as pltpu
from jax.sharding import PartitionSpec as P

STEPS = 8
PMLW = 8
CAND_GX = ("cand", "gx")
CHIPS_X = 4
MESH = pl.DeviceIdType.MESH

step_dt = 0.7
contrast = 5.0
sigma_max = 2.0
small_eps = 1e-06
inv_spacing = 0.5

WIN = 4
WINDOWS = STEPS // WIN
LEFT = 3
FRAME = 9
HALO = 8


def kernel(
    planes, waves, prof, e_in, h_in, den_in, mask_in,
    e_out, h_out, g_out,
    we, wh, fe, fh, send_h, send_e, recv_h, recv_e, ce, src, den, mask, grad, hist, part1, part2,
    load_sem, halo_send, halo_recv, mat_send, mat_recv,
    right_send, right_recv, left_send, left_recv,
    sum1_send, sum1_recv, sum2_send, sum2_recv,
):
    width, own_rows = den.shape[0], den.shape[1]
    rows, depth = own_rows + HALO, den.shape[2]
    count_x = lax.axis_size("gx")
    count_z = count_x // CHIPS_X
    gx, gy = lax.axis_index("gx"), lax.axis_index("gy")
    chip_x, chip_z = gx // count_z, lax.rem(gx, count_z)
    other = 1 - gy
    right = {"gx": lax.rem(gx + 1, count_x), "gy": gy}
    left = {"gx": lax.rem(gx + count_x - 1, count_x), "gy": gy}
    across = {"gx": gx, "gy": other}
    plane_peers = []
    for dx in range(CHIPS_X):
        for dc in range(2):
            if dx or dc:
                peer = lax.rem(chip_x + dx, CHIPS_X) * count_z + chip_z
                plane_peers.append({"gx": peer, "gy": other if dc else gy})
    line_peers = [
        {"gx": chip_x * count_z + lax.rem(chip_z + dz, count_z), "gy": gy}
        for dz in range(1, count_z)
    ]
    own = pl.multiple_of(gy * HALO, HALO)
    top = pl.multiple_of((1 - gy) * (own_rows - HALO), HALO)
    there = pl.multiple_of(gy * own_rows, HALO)
    X0 = LEFT
    block = pl.ds(X0, width)

    loads = [
        pltpu.make_async_copy(den_in, den, load_sem.at[0]),
        pltpu.make_async_copy(mask_in, mask, load_sem.at[1]),
        pltpu.make_async_copy(e_in, we.at[:, :, block, pl.ds(own, own_rows), :], load_sem.at[2]),
        pltpu.make_async_copy(
            h_in, wh.at[:, :, block, pl.ds(own + HALO, own_rows), :], load_sem.at[3]
        ),
    ]
    for load in loads:
        load.start()

    barrier = pltpu.get_barrier_semaphore()
    peers = [left, right] + plane_peers + line_peers
    for peer in peers:
        pl.semaphore_signal(barrier, inc=1, device_id=peer, device_id_type=MESH)

    lanes = lax.broadcasted_iota(jnp.int32, (1, depth), 1)
    zpos = lanes.astype(jnp.float32)
    lower = (PMLW - zpos - 0.5) / PMLW
    upper = (zpos + 0.5 - (depth - PMLW)) / PMLW
    deep = jnp.maximum(jnp.maximum(lower, upper), 0.0)
    half = sigma_max * deep * deep * deep * step_dt / 2.0
    decay1 = (1.0 - half) / (1.0 + half)
    gain1 = step_dt / (1.0 + half)
    decay = jnp.broadcast_to(decay1, (rows, depth))
    gain = jnp.broadcast_to(gain1, (rows, depth))
    gain_half = gain * inv_spacing
    first_lane = jnp.broadcast_to(lanes == 0, (rows, depth))
    last_lane = jnp.broadcast_to(lanes == depth - 1, (rows, depth))
    on_left = (gx > 0).astype(jnp.float32)
    on_right = (gx < count_x - 1).astype(jnp.float32)

    eye = lax.broadcasted_iota(jnp.int32, (own_rows, own_rows), 0) == lax.broadcasted_iota(
        jnp.int32, (own_rows, own_rows), 1
    )
    for s in range(2):
        spot = jnp.where(lanes == planes[s], gain1, 0.0)
        for x in range(width):
            row = jnp.broadcast_to(prof[s, x : x + 1, :], (own_rows, own_rows))
            column = jnp.sum(jnp.where(eye, row, 0.0), axis=1, keepdims=True)
            src[s, x, pl.ds(own, own_rows), :] = column * spot

    pad = jnp.zeros((HALO, depth), jnp.float32)
    plane0 = jnp.zeros((rows, depth), jnp.float32)
    for s in range(2):
        for c in range(3):
            for p in range(FRAME):
                if c != 1:
                    we[s, c, p, rows : rows + HALO, :] = pad
                    wh[s, c, p, 0:HALO, :] = pad
            wh[s, c, 0, HALO:, :] = plane0
    for c in (0, 2):
        for p in range(width + 1):
            fe[c, p, rows : rows + HALO, :] = pad
            fh[c, p, 0:HALO, :] = pad
    for c in range(3):
        fe[c, width, 0:rows, :] = plane0
        fh[c, 0, HALO:, :] = plane0

    pl.semaphore_wait(barrier, len(peers))

    halos = [
        pltpu.make_async_remote_copy(
            e_in.at[:, :, :, pl.ds(top, HALO), :],
            we.at[:, :, block, pl.ds(there, HALO), :],
            halo_send.at[0], halo_recv.at[0], device_id=across, device_id_type=MESH,
        ),
        pltpu.make_async_remote_copy(
            h_in.at[:, :, :, pl.ds(top, HALO), :],
            wh.at[:, :, block, pl.ds(there + HALO, HALO), :],
            halo_send.at[1], halo_recv.at[1], device_id=across, device_id_type=MESH,
        ),
        pltpu.make_async_remote_copy(
            src.at[:, :, pl.ds(pl.multiple_of(own + top, HALO), HALO), :],
            src.at[:, :, pl.ds(there, HALO), :],
            halo_send.at[2], halo_recv.at[2], device_id=across, device_id_type=MESH,
        ),
        pltpu.make_async_remote_copy(
            ce.at[block, pl.ds(pl.multiple_of(own + top, HALO), HALO), :],
            ce.at[block, pl.ds(there, HALO), :],
            halo_send.at[3], halo_recv.at[3], device_id=across, device_id_type=MESH,
        ),
    ]
    halos[0].start()
    halos[1].start()
    halos[2].start()
    loads[0].wait()
    loads[1].wait()
    for x in range(width):
        flags = mask[x].astype(jnp.float32)
        inv_eps = 1.0 / (1.0 + contrast * den[x] * flags)
        ce[X0 + x, pl.ds(own, own_rows), :] = inv_eps * gain1
        grad[x] = flags * contrast * inv_eps * inv_eps * step_dt
    halos[3].start()
    loads[2].wait()
    loads[3].wait()
    for halo in halos:
        halo.wait()

    materials = [
        pltpu.make_async_remote_copy(
            ce.at[pl.ds(X0 + width - 2, 2)], ce.at[pl.ds(X0 - 2, 2)],
            mat_send.at[0], mat_recv.at[0], device_id=right, device_id_type=MESH,
        ),
        pltpu.make_async_remote_copy(
            ce.at[pl.ds(X0, 2)], ce.at[pl.ds(X0 + width, 2)],
            mat_send.at[1], mat_recv.at[1], device_id=left, device_id_type=MESH,
        ),
    ]

    def to_right(s, w, k):
        return pltpu.make_async_remote_copy(
            send_h.at[s, w, k], recv_h.at[s, w, k],
            right_send.at[s, w, k], right_recv.at[s, w, k], device_id=right, device_id_type=MESH,
        )

    def to_left(s, w, k):
        return pltpu.make_async_remote_copy(
            send_e.at[s, w, k], recv_e.at[s, w, k],
            left_send.at[s, w, k], left_recv.at[s, w, k], device_id=left, device_id_type=MESH,
        )

    def up_z(f):
        return jnp.where(last_lane, 0.0, pltpu.roll(f, depth - 1, 1))

    def down_z(f):
        return jnp.where(first_lane, 0.0, pltpu.roll(f, 1, 1))

    def h_update(h_old, e, e_y, e_x, comps=(0, 1, 2)):
        new = {}
        if 0 in comps:
            new[0] = decay * h_old(0) - gain_half * ((e_y(2) - e[2]) - (up_z(e[1]) - e[1]))
        new[1] = decay * h_old(1) - (gain_half * (up_z(e[0]) - e[0]) - gain * (e_x[2] - e[2]))
        new[2] = decay * h_old(2) - (gain * (e_x[1] - e[1]) - gain_half * (e_y(0) - e[0]))
        return new

    def e_update(e_old, h, h_y, h_x, c, drive):
        cx = c * inv_spacing
        x = decay * e_old(0) + cx * ((h[2] - h_y(2)) - (h[1] - down_z(h[1])))
        if drive is not None:
            x = x - drive
        y = decay * e_old(1) + (cx * (h[0] - down_z(h[0])) - c * (h[2] - h_x[2]))
        z = decay * e_old(2) + (c * (h[1] - h_x[1]) - cx * (h[0] - h_y(0)))
        return {0: x, 1: y, 2: z}

    R0, R1 = slice(0, rows), slice(1, rows + 1)
    H0, HM = slice(HALO, HALO + rows), slice(HALO - 1, HALO + rows - 1)

    def free(s, w):
        for c in (1, 2):
            send_e[s, w, 0, c - 1] = we[s, c, X0, R0, :]
        to_left(s, w, 0).start()
        for k in range(WIN):
            last = k == WIN - 1
            h_planes = [x for x in range(width) if x >= k or x < width - 1 - k]
            if last:
                h_planes = [width - 1]
            for x in h_planes:
                if k == 0:
                    old_h = lambda c, x=x: wh[s, c, X0 + x, H0, :]
                    get_e = lambda c, x, r: we[s, c, X0 + x, r, :]
                else:
                    old_h = lambda c, x=x: fh[c, x + 1, H0, :]
                    get_e = lambda c, x, r: fe[c, x, r, :]
                e = {c: get_e(c, x, R0) for c in range(3)}
                e_x = {
                    c: (get_e(c, x + 1, R0) if x < width - 1 else jnp.zeros_like(e[c]))
                    for c in (1, 2)
                }
                new = h_update(
                    old_h, e, lambda c, x=x: get_e(c, x, R1), e_x, (1, 2) if last else (0, 1, 2)
                )
                if not last:
                    for c in range(3):
                        fh[c, x + 1, H0, :] = new[c]
                if x == width - 1:
                    send_h[s, w, k, 0] = new[1]
                    send_h[s, w, k, 1] = new[2]
            to_right(s, w, k).start()
            if last:
                break
            wave = waves[s, w * WIN + k]
            e_planes = [x for x in range(width) if x >= k + 1 or x < width - 1 - k]
            for x in e_planes:
                if k == 0:
                    old_e = lambda c, x=x: we[s, c, X0 + x, R0, :]
                else:
                    old_e = lambda c, x=x: fe[c, x, R0, :]
                h = {c: fh[c, x + 1, H0, :] for c in range(3)}
                h_x = {c: fh[c, x, H0, :] for c in (1, 2)}
                new = e_update(
                    old_e, h, lambda c, x=x: fh[c, x + 1, HM, :], h_x,
                    ce[X0 + x], src[s, x] * wave,
                )
                for c in range(3):
                    fe[c, x, R0, :] = new[c]
                if x == 0:
                    send_e[s, w, k + 1, 0] = new[1]
                    send_e[s, w, k + 1, 1] = new[2]
            to_left(s, w, k + 1).start()

    def true(s, w):
        for c in range(3):
            for p in (X0 - 2, X0 - 1, X0 + width, X0 + width + 1):
                we[s, c, p, R0, :] = plane0
                wh[s, c, p, H0, :] = plane0
        for k in range(WIN):
            reach = min(k + 1, WIN - k)
            h_lo, h_hi = -reach, width + min(k, WIN - 1 - k)
            e_out_reach = min(k + 1, WIN - 1 - k)
            to_left(s, w, k).wait_recv()
            e_next = None
            for x in range(h_hi - 1, h_lo - 1, -1):
                p = X0 + x
                e = {c: we[s, c, p, R0, :] for c in range(3)}
                if e_next is None:
                    e_x = {c: we[s, c, p + 1, R0, :] for c in (1, 2)}
                else:
                    e_x = e_next
                e_next = e
                if x == width - 1:
                    e_x = {c: (e_x[c] + recv_e[s, w, k, c - 1]) * on_right for c in (1, 2)}
                new = h_update(
                    lambda c: wh[s, c, p, H0, :], e, lambda c: we[s, c, p, R1, :], e_x
                )
                for c in range(3):
                    wh[s, c, p, H0, :] = new[c]
            to_right(s, w, k).wait_recv()
            wave = waves[s, w * WIN + k]
            h_last = None
            for x in range(-e_out_reach, width + e_out_reach):
                p = X0 + x
                h = {c: wh[s, c, p, H0, :] for c in range(3)}
                if h_last is None:
                    h_x = {c: wh[s, c, p - 1, H0, :] for c in (1, 2)}
                else:
                    h_x = h_last
                h_last = h
                if x == 0:
                    h_x = {c: (h_x[c] + recv_h[s, w, k, c - 1]) * on_left for c in (1, 2)}
                inside = 0 <= x < width
                new = e_update(
                    lambda c: we[s, c, p, R0, :], h, lambda c: wh[s, c, p, HM, :], h_x,
                    ce[p], src[s, x] * wave if inside else None,
                )
                for c in range(3):
                    we[s, c, p, R0, :] = new[c]
                    if inside:
                        hist[s, w * WIN + k, c, x] = new[c]

    def start_free(s, carry):
        free(s, 0)
        return carry

    lax.fori_loop(0, 2, start_free, 0)
    for material in materials:
        material.start()
    for material in materials:
        material.wait_recv()

    sum1 = [
        pltpu.make_async_remote_copy(
            part1.at[0], part1.at[1 + n], sum1_send.at[n], sum1_recv.at[n],
            device_id=peer, device_id_type=MESH,
        )
        for n, peer in enumerate(plane_peers)
    ]
    sum2 = [
        pltpu.make_async_remote_copy(
            part2.at[0], part2.at[1 + n], sum2_send.at[n], sum2_recv.at[n],
            device_id=peer, device_id_type=MESH,
        )
        for n, peer in enumerate(line_peers)
    ]
    outs = [
        pltpu.make_async_copy(we.at[:, :, block, pl.ds(own, own_rows), :], e_out, load_sem.at[2]),
        pltpu.make_async_copy(
            wh.at[:, :, block, pl.ds(own + HALO, own_rows), :], h_out, load_sem.at[3]
        ),
        pltpu.make_async_copy(grad, g_out, load_sem.at[0]),
    ]

    def turn(j, carry):
        w, s = j // 2, lax.rem(j, 2)
        true(s, w)

        @pl.when(w == 0)
        def _():
            free(s, 1)

        @pl.when(j == 2)
        def _():
            total = jnp.zeros((own_rows, depth), jnp.float32)
            for c in range(3):
                for x in range(width):
                    e = we[0, c, X0 + x, pl.ds(own, own_rows), :]
                    total = total + e * e
            line = jnp.sum(total, axis=0, keepdims=True)
            part1[0] = jnp.where(lanes == planes[1], line, 0.0)
            for copy in sum1:
                copy.start()

        return carry

    lax.fori_loop(0, 2 * WINDOWS, turn, 0)

    for copy in sum1:
        copy.wait_recv()
    total = part1[0]
    for n in range(len(sum1)):
        total = total + part1[1 + n]
    part2[0] = total
    for copy in sum2:
        copy.start()
    outs[0].start()
    outs[1].start()

    for x in range(width):
        corr = jnp.zeros((own_rows, depth), jnp.float32)
        for k in range(STEPS):
            for c in range(3):
                corr = corr + (
                    hist[0, k, c, x, pl.ds(own, own_rows), :]
                    * hist[1, k, c, x, pl.ds(own, own_rows), :]
                )
        grad[x] = grad[x] * corr

    for copy in sum2:
        copy.wait_recv()
    total = part2[0]
    for n in range(len(sum2)):
        total = total + part2[1 + n]
    cells = count_x * width * lax.axis_size("gy") * own_rows
    power = jnp.sum(total, axis=1, keepdims=True) / cells
    scale = jnp.broadcast_to(1.0 / (power + small_eps), (own_rows, depth))
    for x in range(width):
        grad[x] = grad[x] * scale
    outs[2].start()
    for out in outs:
        out.wait()
    for material in materials:
        material.wait_send()
    for copy in sum1 + sum2:
        copy.wait_send()

    def drain(j, carry):
        w, s = j // 2, lax.rem(j, 2)
        for k in range(WIN):
            to_right(s, w, k).wait_send()
            to_left(s, w, k).wait_send()
        return carry

    lax.fori_loop(0, 2 * WINDOWS, drain, 0)


def shards(electric, magnetic, density, design_mask, planes, profiles, waveforms):
    sets, comps, width, own_rows, depth = electric.shape
    rows = own_rows + HALO
    count_z = lax.axis_size("gx") // CHIPS_X
    f32 = jnp.float32
    vmem, dma = pltpu.VMEM, pltpu.SemaphoreType.DMA
    series = vmem((sets, WINDOWS, WIN, 2, rows, depth), f32)
    any_space = pl.BlockSpec(memory_space=pl.ANY)
    smem_space = pl.BlockSpec(memory_space=pltpu.SMEM)
    return pl.pallas_call(
        kernel,
        out_shape=(
            jax.ShapeDtypeStruct(electric.shape, f32),
            jax.ShapeDtypeStruct(magnetic.shape, f32),
            jax.ShapeDtypeStruct(density.shape, f32),
        ),
        in_specs=[smem_space, smem_space, pl.BlockSpec(memory_space=pltpu.VMEM)] + [any_space] * 4,
        out_specs=(any_space,) * 3,
        scratch_shapes=[
            vmem((sets, comps, FRAME, rows + HALO, depth), f32),
            vmem((sets, comps, FRAME, rows + HALO, depth), f32),
            vmem((comps, width + 1, rows + HALO, depth), f32),
            vmem((comps, width + 1, rows + HALO, depth), f32),
            series, series, series, series,
            vmem((FRAME, rows, depth), f32),
            vmem((sets, width, rows, depth), f32),
            vmem((width, own_rows, depth), f32),
            vmem((width, own_rows, depth), jnp.int32),
            vmem((width, own_rows, depth), f32),
            vmem((sets, STEPS, comps, width, rows, depth), f32),
            vmem((2 * CHIPS_X, 1, depth), f32),
            vmem((count_z, 1, depth), f32),
            dma((4,)), dma((4,)), dma((4,)), dma((2,)), dma((2,)),
            dma((sets, WINDOWS, WIN)), dma((sets, WINDOWS, WIN)),
            dma((sets, WINDOWS, WIN)), dma((sets, WINDOWS, WIN)),
            dma((2 * CHIPS_X - 1,)), dma((2 * CHIPS_X - 1,)),
            dma((count_z - 1,)), dma((count_z - 1,)),
        ],
        compiler_params=pltpu.CompilerParams(collective_id=0, has_side_effects=True),
    )(planes, waveforms, profiles, electric, magnetic, density, design_mask)


def solution(mesh):
    return jax.shard_map(
        shards,
        mesh=mesh,
        in_specs=(
            P(None, None, CAND_GX, "gy", None),
            P(None, None, CAND_GX, "gy", None),
            P(CAND_GX, "gy", None),
            P(CAND_GX, "gy", None),
            P("cand"),
            P(None, CAND_GX, "gy"),
            P(None, "cand"),
        ),
        out_specs=(
            P(None, None, CAND_GX, "gy", None),
            P(None, None, CAND_GX, "gy", None),
            P(CAND_GX, "gy", None),
        ),
        check_vma=False,
    )
```

time: 235 us -> 64.8 us (0.28)
  starting transfers between devices: 106 us -> 0 us
  Pallas kernels: 0 us -> 60.6 us
  blocking collectives: 59.1 us -> 0 us
  waiting for transfers between devices: 26.3 us -> 0 us
  other arithmetic: 24.8 us -> 0 us
  local copies, waits for them, and re-layouts: 13.3 us -> 3.32 us
  between operations: 3.09 us -> 0.65 us
    ppermute x44 -> x0, starting transfers between devices: 106 us -> none  [the longest x22 77 us: with_halo(): lax.ppermute(lax.slice_in_dim(block, block.shape[dim] - width, None, axis...]
    pallas_call x0 -> x1, Pallas kernels: none -> 60.6 us  [shards(): pl.pallas_call(kernel, out_shape=(jax.ShapeDtypeStruct(electric.shape, f3...]
    psum x3 -> x0, blocking collectives: 59.1 us -> none  [over_axes(): x = lax.psum(x, axis)]
    ppermute x44 -> x0, waiting for transfers between devices: 26.3 us -> none  [the longest x22 26.2 us: with_halo(): lax.ppermute(lax.slice_in_dim(block, 0, width, axis=dim), axis, backward)]
    mul x23 -> x0, other arithmetic: 13.9 us -> none  [the longest x2 5.2 us: shards(): source_wide * waveforms[0, step]]
    slice x87 -> x0, local copies, waits for them, and re-layouts: 7.34 us -> none  [the longest x16 2.11 us: fwd_z(): field[..., 1:]]
    another operation x24 -> x0, other arithmetic: 5.31 us -> none  [the longest x16 3.79 us: electric_update(): return jnp.stack([new_x, new_y, new_z], 1)]
  transfers between devices with their start and end apart: 44 -> 0, of which waited for: 12 -> 0; matrix products, arithmetic and copies ran while one was open for 9% -> 0% of each run, Pallas kernels for 0% -> 0%
where the time goes in v1:
time: 64.8 us; the launch traced here: 64.6 us
  Pallas kernels  60.6 us (94%)
  local copies, waits for them, and re-layouts  3.32 us (5%)
  between operations  0.65 us (1%)
    pallas_call x1, Pallas kernels, shards(): pl.pallas_call(kernel, out_shape=(jax.ShapeDtypeStruct(electric.shape, f3...  60.6 us
    unnamed x7, local copies, waits for them, and re-layouts  3.32 us

profile of v1, /device:TPU:40, one launch (start us, length us, event | category | flops | bytes accessed | tf_op | source)
XLA Modules:
  0.0 64.6 jit_solution(18101615325895666443)
XLA Ops:
  0.6 60.6 %shard_map.94 = (f32[2,3,4,32,128]{4,3,2,1,0:T(8,128)}, f32[2,3,4,32,128]{4,3,2,1,0:T(8,128)}, f32[4,32,128]{2,1,0:T(8,128)}) custom-call(s32[2]{0:T(128)} %planes.1, f32[2,8]{1,0:T(2,128)} %waves.1, f32[2,4,32]{2,1,0:T(4,128)} %prof.1, f32[2,3,4,32,128]{4,3,2,1,0:T(8,128)} %e_in.1, f32[2,3,4,32,128]{4,3,2,1,0:T(8,128)} %h_in.1, f32[4,32,128]{2,1,0:T(8,128)} %den_in.1, ...), custom_call_target="tpu_custom_call" | custom-call | tf_op jit(solution)/shard_map/pallas_call | solution.py:425
  61.2 0.0 copy-start
  61.2 1.8 %copy.13 = f32[2,3,4,32,128]{4,3,2,1,0:T(8,128)} copy(f32[2,3,4,32,128]{4,3,2,1,0:T(8,128)} %get-tuple-element.6) | data formatting | bytes 786432
  63.1 0.0 copy-done
  63.1 0.0 copy-start.1
  63.1 0.7 %copy.14 = f32[2,3,4,32,128]{4,3,2,1,0:T(8,128)} copy(f32[2,3,4,32,128]{4,3,2,1,0:T(8,128)S(1)} %copy-done) | data formatting | bytes 786432
  63.8 0.1 copy-done.1
  63.9 0.6 copy.15
Async XLA Ops:
  61.2 1.8 %copy-start = (f32[2,3,4,32,128]{4,3,2,1,0:T(8,128)S(1)}, f32[2,3,4,32,128]{4,3,2,1,0:T(8,128)}, u32[]{:S(2)}) copy-start(f32[2,3,4,32,128]{4,3,2,1,0:T(8,128)} %get-tuple-element.7) | copy-start | bytes 1179652
  63.1 0.9 %copy-start.1 = (f32[4,32,128]{2,1,0:T(8,128)S(1)}, f32[4,32,128]{2,1,0:T(8,128)}, u32[]{:S(2)}) copy-start(f32[4,32,128]{2,1,0:T(8,128)} %get-tuple-element.8) | copy-start | bytes 196612

commit v2 on v1

--- a/solution.py
+++ b/solution.py
@@ -25,10 +25,10 @@
 
 
 def kernel(
-    planes, waves, prof, e_in, h_in, den_in, mask_in,
-    e_out, h_out, g_out,
-    we, wh, fe, fh, send_h, send_e, recv_h, recv_e, ce, src, den, mask, grad, hist, part1, part2,
-    load_sem, halo_send, halo_recv, mat_send, mat_recv,
+    planes_in, waves_in, prof_in, e_in, h_in, den_in, mask_in,
+    we, wh, grad,
+    fe, fh, send_h, send_e, recv_h, recv_e, ce, src, den, mask, hist, part1, part2,
+    planes, waves, prof, load_sem, near, mid, far, halo_send, halo_recv, mat_send, mat_recv,
     right_send, right_recv, left_send, left_recv,
     sum1_send, sum1_recv, sum2_send, sum2_recv,
 ):
@@ -48,9 +48,16 @@
             if dx or dc:
                 peer = lax.rem(chip_x + dx, CHIPS_X) * count_z + chip_z
                 plane_peers.append({"gx": peer, "gy": other if dc else gy})
-    line_peers = [
-        {"gx": chip_x * count_z + lax.rem(chip_z + dz, count_z), "gy": gy}
-        for dz in range(1, count_z)
+
+    def along_z(dz):
+        return {"gx": chip_x * count_z + lax.rem(chip_z + dz, count_z), "gy": gy}
+
+    def both_ways(d):
+        return [along_z(dz) for dz in sorted({d % count_z, -d % count_z} - {0})]
+
+    line_peers = [along_z(dz) for dz in range(1, count_z)]
+    next_chips = [
+        {"gx": lax.rem(chip_x + dx, CHIPS_X) * count_z + chip_z, "gy": gy} for dx in (1, CHIPS_X - 1)
     ]
     own = pl.multiple_of(gy * HALO, HALO)
     top = pl.multiple_of((1 - gy) * (own_rows - HALO), HALO)
@@ -65,14 +72,23 @@
         pltpu.make_async_copy(
             h_in, wh.at[:, :, block, pl.ds(own + HALO, own_rows), :], load_sem.at[3]
         ),
+        pltpu.make_async_copy(planes_in, planes, load_sem.at[4]),
+        pltpu.make_async_copy(waves_in, waves, load_sem.at[5]),
+        pltpu.make_async_copy(prof_in, prof, load_sem.at[6]),
     ]
     for load in loads:
         load.start()
 
+    def signal(semaphore, peers):
+        for peer in peers:
+            pl.semaphore_signal(semaphore, inc=1, device_id=peer, device_id_type=MESH)
+
     barrier = pltpu.get_barrier_semaphore()
-    peers = [left, right] + plane_peers + line_peers
-    for peer in peers:
-        pl.semaphore_signal(barrier, inc=1, device_id=peer, device_id_type=MESH)
+    peers = [across, left, right] + next_chips + both_ways(1)
+    near_peers = next_chips + both_ways(1)
+    mid_peers = next_chips + both_ways(2)
+    far_peers = both_ways(4)
+    signal(barrier, peers)
 
     lanes = lax.broadcasted_iota(jnp.int32, (1, depth), 1)
     zpos = lanes.astype(jnp.float32)
@@ -93,6 +109,8 @@
     eye = lax.broadcasted_iota(jnp.int32, (own_rows, own_rows), 0) == lax.broadcasted_iota(
         jnp.int32, (own_rows, own_rows), 1
     )
+    loads[4].wait()
+    loads[6].wait()
     for s in range(2):
         spot = jnp.where(lanes == planes[s], gain1, 0.0)
         for x in range(width):
@@ -118,6 +136,7 @@
         fh[c, 0, HALO:, :] = plane0
 
     pl.semaphore_wait(barrier, len(peers))
+    signal(near, near_peers)
 
     halos = [
         pltpu.make_async_remote_copy(
@@ -154,6 +173,7 @@
     halos[3].start()
     loads[2].wait()
     loads[3].wait()
+    loads[5].wait()
     for halo in halos:
         halo.wait()
 
@@ -259,7 +279,7 @@
                     send_e[s, w, k + 1, 1] = new[2]
             to_left(s, w, k + 1).start()
 
-    def true(s, w):
+    def true(s, w, before_last):
         for c in range(3):
             for p in (X0 - 2, X0 - 1, X0 + width, X0 + width + 1):
                 we[s, c, p, R0, :] = plane0
@@ -268,6 +288,8 @@
             reach = min(k + 1, WIN - k)
             h_lo, h_hi = -reach, width + min(k, WIN - 1 - k)
             e_out_reach = min(k + 1, WIN - 1 - k)
+            if k == WIN - 1:
+                before_last()
             to_left(s, w, k).wait_recv()
             e_next = None
             for x in range(h_hi - 1, h_lo - 1, -1):
@@ -313,6 +335,8 @@
         return carry
 
     lax.fori_loop(0, 2, start_free, 0)
+    pl.semaphore_wait(near, len(near_peers))
+    signal(mid, mid_peers)
     for material in materials:
         material.start()
     for material in materials:
@@ -332,24 +356,35 @@
         )
         for n, peer in enumerate(line_peers)
     ]
-    outs = [
-        pltpu.make_async_copy(we.at[:, :, block, pl.ds(own, own_rows), :], e_out, load_sem.at[2]),
-        pltpu.make_async_copy(
-            wh.at[:, :, block, pl.ds(own + HALO, own_rows), :], h_out, load_sem.at[3]
-        ),
-        pltpu.make_async_copy(grad, g_out, load_sem.at[0]),
-    ]
-
     def turn(j, carry):
         w, s = j // 2, lax.rem(j, 2)
-        true(s, w)
+
+        def add_plane():
+            @pl.when(j == 3)
+            def _():
+                for copy in sum1:
+                    copy.wait_recv()
+                total = part1[0]
+                for n in range(len(sum1)):
+                    total = total + part1[1 + n]
+                part2[0] = total
+                for copy in sum2:
+                    copy.start()
+
+        true(s, w, add_plane)
 
         @pl.when(w == 0)
         def _():
             free(s, 1)
 
+        @pl.when(j == 1)
+        def _():
+            pl.semaphore_wait(mid, len(mid_peers))
+            signal(far, far_peers)
+
         @pl.when(j == 2)
         def _():
+            pl.semaphore_wait(far, len(far_peers))
             total = jnp.zeros((own_rows, depth), jnp.float32)
             for c in range(3):
                 for x in range(width):
@@ -363,17 +398,6 @@
         return carry
 
     lax.fori_loop(0, 2 * WINDOWS, turn, 0)
-
-    for copy in sum1:
-        copy.wait_recv()
-    total = part1[0]
-    for n in range(len(sum1)):
-        total = total + part1[1 + n]
-    part2[0] = total
-    for copy in sum2:
-        copy.start()
-    outs[0].start()
-    outs[1].start()
 
     for x in range(width):
         corr = jnp.zeros((own_rows, depth), jnp.float32)
@@ -395,9 +419,6 @@
     scale = jnp.broadcast_to(1.0 / (power + small_eps), (own_rows, depth))
     for x in range(width):
         grad[x] = grad[x] * scale
-    outs[2].start()
-    for out in outs:
-        out.wait()
     for material in materials:
         material.wait_send()
     for copy in sum1 + sum2:
@@ -411,6 +432,29 @@
         return carry
 
     lax.fori_loop(0, 2 * WINDOWS, drain, 0)
+
+
+def store(we, wh, grad, e_out, h_out, g_out, sem):
+    width, own_rows = grad.shape[0], grad.shape[1]
+    own = pl.multiple_of(lax.axis_index("gy") * HALO, HALO)
+    block = pl.ds(LEFT, width)
+    outs = [
+        pltpu.make_async_copy(we.at[:, :, block, pl.ds(own, own_rows), :], e_out, sem.at[0]),
+        pltpu.make_async_copy(wh.at[:, :, block, pl.ds(own + HALO, own_rows), :], h_out, sem.at[1]),
+        pltpu.make_async_copy(grad, g_out, sem.at[2]),
+    ]
+    for out in outs:
+        out.start()
+    for out in outs:
+        out.wait()
+
+
+def vmem_array(shape):
+    return pltpu.VMEM(shape, jnp.float32)
+
+
+def in_vmem(x):
+    return pltpu.with_memory_space_constraint(x, pltpu.VMEM)
 
 
 def shards(electric, magnetic, density, design_mask, planes, profiles, waveforms):
@@ -421,19 +465,15 @@
     vmem, dma = pltpu.VMEM, pltpu.SemaphoreType.DMA
     series = vmem((sets, WINDOWS, WIN, 2, rows, depth), f32)
     any_space = pl.BlockSpec(memory_space=pl.ANY)
-    smem_space = pl.BlockSpec(memory_space=pltpu.SMEM)
-    return pl.pallas_call(
+    held = pl.BlockSpec(memory_space=pltpu.VMEM)
+    smem, wait = pltpu.SMEM, pltpu.SemaphoreType.REGULAR
+    frame = (sets, comps, FRAME, rows + HALO, depth)
+    e_frame, h_frame, grad = pl.pallas_call(
         kernel,
-        out_shape=(
-            jax.ShapeDtypeStruct(electric.shape, f32),
-            jax.ShapeDtypeStruct(magnetic.shape, f32),
-            jax.ShapeDtypeStruct(density.shape, f32),
-        ),
-        in_specs=[smem_space, smem_space, pl.BlockSpec(memory_space=pltpu.VMEM)] + [any_space] * 4,
-        out_specs=(any_space,) * 3,
+        out_shape=(vmem_array(frame), vmem_array(frame), vmem_array(density.shape)),
+        in_specs=[any_space] * 7,
+        out_specs=(held,) * 3,
         scratch_shapes=[
-            vmem((sets, comps, FRAME, rows + HALO, depth), f32),
-            vmem((sets, comps, FRAME, rows + HALO, depth), f32),
             vmem((comps, width + 1, rows + HALO, depth), f32),
             vmem((comps, width + 1, rows + HALO, depth), f32),
             series, series, series, series,
@@ -441,18 +481,34 @@
             vmem((sets, width, rows, depth), f32),
             vmem((width, own_rows, depth), f32),
             vmem((width, own_rows, depth), jnp.int32),
-            vmem((width, own_rows, depth), f32),
             vmem((sets, STEPS, comps, width, rows, depth), f32),
             vmem((2 * CHIPS_X, 1, depth), f32),
             vmem((count_z, 1, depth), f32),
-            dma((4,)), dma((4,)), dma((4,)), dma((2,)), dma((2,)),
+            smem(planes.shape, jnp.int32),
+            smem(waveforms.shape, f32),
+            vmem(profiles.shape, f32),
+            dma((7,)), wait, wait, wait, dma((4,)), dma((4,)), dma((2,)), dma((2,)),
             dma((sets, WINDOWS, WIN)), dma((sets, WINDOWS, WIN)),
             dma((sets, WINDOWS, WIN)), dma((sets, WINDOWS, WIN)),
             dma((2 * CHIPS_X - 1,)), dma((2 * CHIPS_X - 1,)),
-            dma((count_z - 1,)), dma((count_z - 1,)),
+            dma((max(count_z - 1, 1),)), dma((max(count_z - 1, 1),)),
         ],
-        compiler_params=pltpu.CompilerParams(collective_id=0, has_side_effects=True),
+        compiler_params=pltpu.CompilerParams(
+            collective_id=0, has_side_effects=True, vmem_limit_bytes=64_200_000
+        ),
     )(planes, waveforms, profiles, electric, magnetic, density, design_mask)
+    return pl.pallas_call(
+        store,
+        out_shape=(
+            jax.ShapeDtypeStruct(electric.shape, f32),
+            jax.ShapeDtypeStruct(magnetic.shape, f32),
+            jax.ShapeDtypeStruct(density.shape, f32),
+        ),
+        in_specs=[held] * 3,
+        out_specs=(any_space,) * 3,
+        scratch_shapes=[dma((3,))],
+        compiler_params=pltpu.CompilerParams(vmem_limit_bytes=4 << 20),
+    )(in_vmem(e_frame), in_vmem(h_frame), in_vmem(grad))
 
 
 def solution(mesh):

time: 64.8 us -> 57.4 us (0.89)
  Pallas kernels: 60.6 us -> 56.7 us
  local copies, waits for them, and re-layouts: 3.32 us -> 0 us
    pallas_call x1 -> x2, Pallas kernels: 60.6 us -> 56.7 us  [the longest x1 55.7 us: shards(): pl.pallas_call(kernel, out_shape=(vmem_array(frame), vmem_array(frame), v...]
    unnamed x7 -> x0, local copies, waits for them, and re-layouts: 3.32 us -> none
where the time goes in v2:
time: 57.4 us; the launch traced here: 57.3 us
  Pallas kernels  56.7 us (99%)
  between operations  0.64 us (1%)
    pallas_call x1, Pallas kernels, shards(): pl.pallas_call(kernel, out_shape=(vmem_array(frame), vmem_array(frame), v...  55.7 us

profile of v2, /device:TPU:40, one launch (start us, length us, event | category | flops | bytes accessed | tf_op | source)
XLA Modules:
  0.0 57.3 jit_solution(6351080271754081787)
XLA Ops:
  0.6 55.7 %shard_map.94 = (f32[2,3,9,48,128]{4,3,2,1,0:T(8,128)S(1)}, f32[2,3,9,48,128]{4,3,2,1,0:T(8,128)S(1)}, f32[4,32,128]{2,1,0:T(8,128)S(1)}) custom-call(s32[2]{0:T(128)} %planes_in.1, f32[2,8]{1,0:T(2,128)} %waves_in.1, f32[2,4,32]{2,1,0:T(4,128)} %prof_in.1, f32[2,3,4,32,128]{4,3,2,1,0:T(8,128)} %e_in.1, f32[2,3,4,32,128]{4,3,2,1,0:T(8,128)} %h_in.1, ...), custom_call_target="tpu_custom_call" | custom-call | tf_op jit(solution)/shard_map/pallas_call | solution.py:471
  56.4 0.9 %shard_map.95 = (f32[2,3,4,32,128]{4,3,2,1,0:T(8,128)}, f32[2,3,4,32,128]{4,3,2,1,0:T(8,128)}, f32[4,32,128]{2,1,0:T(8,128)}) custom-call(f32[2,3,9,48,128]{4,3,2,1,0:T(8,128)S(1)} %get-tuple-element.6.we, f32[2,3,9,48,128]{4,3,2,1,0:T(8,128)S(1)} %get-tuple-element.7.wh, f32[4,32,128]{2,1,0:T(8,128)S(1)} %get-tuple-element.8.grad), custom_call_target="tpu_custom_call" | custom-call | tf_op jit(solution)/shard_map/pallas_call | solution.py:500

commit v3 on v2

--- a/solution.py
+++ b/solution.py
@@ -42,6 +42,8 @@
     right = {"gx": lax.rem(gx + 1, count_x), "gy": gy}
     left = {"gx": lax.rem(gx + count_x - 1, count_x), "gy": gy}
     across = {"gx": gx, "gy": other}
+    right_across, left_across = dict(right, gy=other), dict(left, gy=other)
+    has_right, has_left = gx < count_x - 1, gx > 0
     plane_peers = []
     for dx in range(CHIPS_X):
         for dc in range(2):
@@ -84,7 +86,7 @@
             pl.semaphore_signal(semaphore, inc=1, device_id=peer, device_id_type=MESH)
 
     barrier = pltpu.get_barrier_semaphore()
-    peers = [across, left, right] + next_chips + both_ways(1)
+    peers = [across, left, right, left_across, right_across] + next_chips + both_ways(1)
     near_peers = next_chips + both_ways(1)
     mid_peers = next_chips + both_ways(2)
     far_peers = both_ways(4)
@@ -103,20 +105,8 @@
     gain_half = gain * inv_spacing
     first_lane = jnp.broadcast_to(lanes == 0, (rows, depth))
     last_lane = jnp.broadcast_to(lanes == depth - 1, (rows, depth))
-    on_left = (gx > 0).astype(jnp.float32)
-    on_right = (gx < count_x - 1).astype(jnp.float32)
-
-    eye = lax.broadcasted_iota(jnp.int32, (own_rows, own_rows), 0) == lax.broadcasted_iota(
-        jnp.int32, (own_rows, own_rows), 1
-    )
-    loads[4].wait()
-    loads[6].wait()
-    for s in range(2):
-        spot = jnp.where(lanes == planes[s], gain1, 0.0)
-        for x in range(width):
-            row = jnp.broadcast_to(prof[s, x : x + 1, :], (own_rows, own_rows))
-            column = jnp.sum(jnp.where(eye, row, 0.0), axis=1, keepdims=True)
-            src[s, x, pl.ds(own, own_rows), :] = column * spot
+    on_left = has_left.astype(jnp.float32)
+    on_right = has_right.astype(jnp.float32)
 
     pad = jnp.zeros((HALO, depth), jnp.float32)
     plane0 = jnp.zeros((rows, depth), jnp.float32)
@@ -135,8 +125,19 @@
         fe[c, width, 0:rows, :] = plane0
         fh[c, 0, HALO:, :] = plane0
 
+    @pl.when(jnp.logical_not(has_right))
+    def _():
+        recv_e[...] = jnp.zeros_like(recv_e)
+        for p in (X0 + width, X0 + width + 1):
+            ce[p] = plane0
+
+    @pl.when(jnp.logical_not(has_left))
+    def _():
+        recv_h[...] = jnp.zeros_like(recv_h)
+        for p in (X0 - 2, X0 - 1):
+            ce[p] = plane0
+
     pl.semaphore_wait(barrier, len(peers))
-    signal(near, near_peers)
 
     halos = [
         pltpu.make_async_remote_copy(
@@ -162,31 +163,66 @@
     ]
     halos[0].start()
     halos[1].start()
-    halos[2].start()
+
+    own_slice = pl.ds(own, own_rows)
+    halo_slice = pl.ds(pl.multiple_of(own + top, HALO), HALO)
+    there_slice = pl.ds(there, HALO)
+    high, low = pl.ds(X0 + width - 2, 2), pl.ds(X0, 2)
+    high_ghost, low_ghost = pl.ds(X0 + width, 2), pl.ds(X0 - 2, 2)
+
+    def material(n, planes_from, planes_to, rows_from, rows_to, device):
+        return pltpu.make_async_remote_copy(
+            ce.at[planes_from, rows_from], ce.at[planes_to, rows_to],
+            mat_send.at[n], mat_recv.at[n], device_id=device, device_id_type=MESH,
+        )
+
+    go_right = [
+        material(0, high, low_ghost, own_slice, own_slice, right),
+        material(1, high, low_ghost, halo_slice, there_slice, right_across),
+    ]
+    go_left = [
+        material(2, low, high_ghost, own_slice, own_slice, left),
+        material(3, low, high_ghost, halo_slice, there_slice, left_across),
+    ]
+
+    def each(condition, action):
+        @pl.when(condition)
+        def _():
+            action()
+
+    def start_all(copies):
+        for copy in copies:
+            copy.start()
+
     loads[0].wait()
     loads[1].wait()
     for x in range(width):
         flags = mask[x].astype(jnp.float32)
         inv_eps = 1.0 / (1.0 + contrast * den[x] * flags)
-        ce[X0 + x, pl.ds(own, own_rows), :] = inv_eps * gain1
+        ce[X0 + x, own_slice, :] = inv_eps * gain1
         grad[x] = flags * contrast * inv_eps * inv_eps * step_dt
     halos[3].start()
+    each(has_right, lambda: start_all(go_right))
+    each(has_left, lambda: start_all(go_left))
+    eye = lax.broadcasted_iota(jnp.int32, (own_rows, own_rows), 0) == lax.broadcasted_iota(
+        jnp.int32, (own_rows, own_rows), 1
+    )
+    loads[4].wait()
+    loads[6].wait()
+    for s in range(2):
+        spot = jnp.where(lanes == planes[s], gain1, 0.0)
+        for x in range(width):
+            row = jnp.broadcast_to(prof[s, x : x + 1, :], (own_rows, own_rows))
+            column = jnp.sum(jnp.where(eye, row, 0.0), axis=1, keepdims=True)
+            src[s, x, pl.ds(own, own_rows), :] = column * spot
+
+    halos[2].start()
+    signal(near, near_peers)
     loads[2].wait()
     loads[3].wait()
     loads[5].wait()
     for halo in halos:
         halo.wait()
-
-    materials = [
-        pltpu.make_async_remote_copy(
-            ce.at[pl.ds(X0 + width - 2, 2)], ce.at[pl.ds(X0 - 2, 2)],
-            mat_send.at[0], mat_recv.at[0], device_id=right, device_id_type=MESH,
-        ),
-        pltpu.make_async_remote_copy(
-            ce.at[pl.ds(X0, 2)], ce.at[pl.ds(X0 + width, 2)],
-            mat_send.at[1], mat_recv.at[1], device_id=left, device_id_type=MESH,
-        ),
-    ]
 
     def to_right(s, w, k):
         return pltpu.make_async_remote_copy(
@@ -229,7 +265,7 @@
     def free(s, w):
         for c in (1, 2):
             send_e[s, w, 0, c - 1] = we[s, c, X0, R0, :]
-        to_left(s, w, 0).start()
+        each(has_left, lambda: to_left(s, w, 0).start())
         for k in range(WIN):
             last = k == WIN - 1
             h_planes = [x for x in range(width) if x >= k or x < width - 1 - k]
@@ -256,7 +292,7 @@
                 if x == width - 1:
                     send_h[s, w, k, 0] = new[1]
                     send_h[s, w, k, 1] = new[2]
-            to_right(s, w, k).start()
+            each(has_right, lambda: to_right(s, w, k).start())
             if last:
                 break
             wave = waves[s, w * WIN + k]
@@ -277,9 +313,9 @@
                 if x == 0:
                     send_e[s, w, k + 1, 0] = new[1]
                     send_e[s, w, k + 1, 1] = new[2]
-            to_left(s, w, k + 1).start()
-
-    def true(s, w, before_last):
+            each(has_left, lambda: to_left(s, w, k + 1).start())
+
+    def true(s, w, relay):
         for c in range(3):
             for p in (X0 - 2, X0 - 1, X0 + width, X0 + width + 1):
                 we[s, c, p, R0, :] = plane0
@@ -288,9 +324,9 @@
             reach = min(k + 1, WIN - k)
             h_lo, h_hi = -reach, width + min(k, WIN - 1 - k)
             e_out_reach = min(k + 1, WIN - 1 - k)
-            if k == WIN - 1:
-                before_last()
-            to_left(s, w, k).wait_recv()
+            if k == WIN - 2:
+                relay()
+            each(has_right, lambda: to_left(s, w, k).wait_recv())
             e_next = None
             for x in range(h_hi - 1, h_lo - 1, -1):
                 p = X0 + x
@@ -307,7 +343,7 @@
                 )
                 for c in range(3):
                     wh[s, c, p, H0, :] = new[c]
-            to_right(s, w, k).wait_recv()
+            each(has_left, lambda: to_right(s, w, k).wait_recv())
             wave = waves[s, w * WIN + k]
             h_last = None
             for x in range(-e_out_reach, width + e_out_reach):
@@ -337,10 +373,17 @@
     lax.fori_loop(0, 2, start_free, 0)
     pl.semaphore_wait(near, len(near_peers))
     signal(mid, mid_peers)
-    for material in materials:
-        material.start()
-    for material in materials:
-        material.wait_recv()
+
+    def wait_recvs(copies):
+        for copy in copies:
+            copy.wait_recv()
+
+    def wait_sends(copies):
+        for copy in copies:
+            copy.wait_send()
+
+    each(has_left, lambda: wait_recvs(go_right))
+    each(has_right, lambda: wait_recvs(go_left))
 
     sum1 = [
         pltpu.make_async_remote_copy(
@@ -419,16 +462,16 @@
     scale = jnp.broadcast_to(1.0 / (power + small_eps), (own_rows, depth))
     for x in range(width):
         grad[x] = grad[x] * scale
-    for material in materials:
-        material.wait_send()
+    each(has_right, lambda: wait_sends(go_right))
+    each(has_left, lambda: wait_sends(go_left))
     for copy in sum1 + sum2:
         copy.wait_send()
 
     def drain(j, carry):
         w, s = j // 2, lax.rem(j, 2)
         for k in range(WIN):
-            to_right(s, w, k).wait_send()
-            to_left(s, w, k).wait_send()
+            each(has_right, lambda: to_right(s, w, k).wait_send())
+            each(has_left, lambda: to_left(s, w, k).wait_send())
         return carry
 
     lax.fori_loop(0, 2 * WINDOWS, drain, 0)
@@ -487,7 +530,7 @@
             smem(planes.shape, jnp.int32),
             smem(waveforms.shape, f32),
             vmem(profiles.shape, f32),
-            dma((7,)), wait, wait, wait, dma((4,)), dma((4,)), dma((2,)), dma((2,)),
+            dma((7,)), wait, wait, wait, dma((4,)), dma((4,)), dma((4,)), dma((4,)),
             dma((sets, WINDOWS, WIN)), dma((sets, WINDOWS, WIN)),
             dma((sets, WINDOWS, WIN)), dma((sets, WINDOWS, WIN)),
             dma((2 * CHIPS_X - 1,)), dma((2 * CHIPS_X - 1,)),

time: 57.4 us -> 52.8 us (0.920)
  Pallas kernels: 56.7 us -> 52.1 us
    pallas_call x1, Pallas kernels: 55.7 us -> 51.1 us  [shards(): pl.pallas_call(kernel, out_shape=(vmem_array(frame), vmem_array(frame), v...]
where the time goes in v3:
time: 52.8 us; the launch traced here: 52.7 us
  Pallas kernels  52.1 us (99%)
  between operations  0.64 us (1%)
    pallas_call x1, Pallas kernels, shards(): pl.pallas_call(kernel, out_shape=(vmem_array(frame), vmem_array(frame), v...  51.1 us

profile of v3, /device:TPU:40, one launch (start us, length us, event | category | flops | bytes accessed | tf_op | source)
XLA Modules:
  0.0 52.7 jit_solution(12272696406661567220)
XLA Ops:
  0.6 51.1 %shard_map.94 = (f32[2,3,9,48,128]{4,3,2,1,0:T(8,128)S(1)}, f32[2,3,9,48,128]{4,3,2,1,0:T(8,128)S(1)}, f32[4,32,128]{2,1,0:T(8,128)S(1)}) custom-call(s32[2]{0:T(128)} %planes_in.1, f32[2,8]{1,0:T(2,128)} %waves_in.1, f32[2,4,32]{2,1,0:T(4,128)} %prof_in.1, f32[2,3,4,32,128]{4,3,2,1,0:T(8,128)} %e_in.1, f32[2,3,4,32,128]{4,3,2,1,0:T(8,128)} %h_in.1, ...), custom_call_target="tpu_custom_call" | custom-call | tf_op jit(solution)/shard_map/pallas_call | solution.py:514
  51.8 0.9 %shard_map.95 = (f32[2,3,4,32,128]{4,3,2,1,0:T(8,128)}, f32[2,3,4,32,128]{4,3,2,1,0:T(8,128)}, f32[4,32,128]{2,1,0:T(8,128)}) custom-call(f32[2,3,9,48,128]{4,3,2,1,0:T(8,128)S(1)} %get-tuple-element.6.we, f32[2,3,9,48,128]{4,3,2,1,0:T(8,128)S(1)} %get-tuple-element.7.wh, f32[4,32,128]{2,1,0:T(8,128)S(1)} %get-tuple-element.8.grad), custom_call_target="tpu_custom_call" | custom-call | tf_op jit(solution)/shard_map/pallas_call | solution.py:543

commit v4 on v3

--- a/solution.py
+++ b/solution.py
@@ -27,7 +27,7 @@
 def kernel(
     planes_in, waves_in, prof_in, e_in, h_in, den_in, mask_in,
     we, wh, grad,
-    fe, fh, send_h, send_e, recv_h, recv_e, ce, src, den, mask, hist, part1, part2,
+    fe, fh, pe, ph, send_h, send_e, recv_h, recv_e, ce, src, den, mask, hist, part1, part2,
     planes, waves, prof, load_sem, near, mid, far, halo_send, halo_recv, mat_send, mat_recv,
     right_send, right_recv, left_send, left_recv,
     sum1_send, sum1_recv, sum2_send, sum2_recv,
@@ -57,7 +57,9 @@
     def both_ways(d):
         return [along_z(dz) for dz in sorted({d % count_z, -d % count_z} - {0})]
 
-    line_peers = [along_z(dz) for dz in range(1, count_z)]
+    line_peers = [
+        along_z(dz) for dz in sorted(range(1, count_z), key=lambda d: -min(d, count_z - d))
+    ]
     next_chips = [
         {"gx": lax.rem(chip_x + dx, CHIPS_X) * count_z + chip_z, "gy": gy} for dx in (1, CHIPS_X - 1)
     ]
@@ -67,6 +69,7 @@
     X0 = LEFT
     block = pl.ds(X0, width)
 
+    early_rows = pl.ds(HALO, own_rows)
     loads = [
         pltpu.make_async_copy(den_in, den, load_sem.at[0]),
         pltpu.make_async_copy(mask_in, mask, load_sem.at[1]),
@@ -77,6 +80,8 @@
         pltpu.make_async_copy(planes_in, planes, load_sem.at[4]),
         pltpu.make_async_copy(waves_in, waves, load_sem.at[5]),
         pltpu.make_async_copy(prof_in, prof, load_sem.at[6]),
+        pltpu.make_async_copy(e_in.at[0], pe.at[:, pl.ds(0, width), early_rows], load_sem.at[7]),
+        pltpu.make_async_copy(h_in.at[0], ph.at[:, pl.ds(1, width), early_rows], load_sem.at[8]),
     ]
     for load in loads:
         load.start()
@@ -100,11 +105,7 @@
     half = sigma_max * deep * deep * deep * step_dt / 2.0
     decay1 = (1.0 - half) / (1.0 + half)
     gain1 = step_dt / (1.0 + half)
-    decay = jnp.broadcast_to(decay1, (rows, depth))
-    gain = jnp.broadcast_to(gain1, (rows, depth))
-    gain_half = gain * inv_spacing
-    first_lane = jnp.broadcast_to(lanes == 0, (rows, depth))
-    last_lane = jnp.broadcast_to(lanes == depth - 1, (rows, depth))
+    gain_half1 = gain1 * inv_spacing
     on_left = has_left.astype(jnp.float32)
     on_right = has_right.astype(jnp.float32)
 
@@ -121,9 +122,12 @@
         for p in range(width + 1):
             fe[c, p, rows : rows + HALO, :] = pad
             fh[c, p, 0:HALO, :] = pad
+            pe[c, p, rows : rows + HALO, :] = pad
+            ph[c, p, 0:HALO, :] = pad
     for c in range(3):
         fe[c, width, 0:rows, :] = plane0
         fh[c, 0, HALO:, :] = plane0
+        ph[c, 0, HALO:, :] = plane0
 
     @pl.when(jnp.logical_not(has_right))
     def _():
@@ -138,35 +142,34 @@
             ce[p] = plane0
 
     pl.semaphore_wait(barrier, len(peers))
-
-    halos = [
-        pltpu.make_async_remote_copy(
-            e_in.at[:, :, :, pl.ds(top, HALO), :],
-            we.at[:, :, block, pl.ds(there, HALO), :],
-            halo_send.at[0], halo_recv.at[0], device_id=across, device_id_type=MESH,
-        ),
-        pltpu.make_async_remote_copy(
-            h_in.at[:, :, :, pl.ds(top, HALO), :],
-            wh.at[:, :, block, pl.ds(there + HALO, HALO), :],
-            halo_send.at[1], halo_recv.at[1], device_id=across, device_id_type=MESH,
-        ),
-        pltpu.make_async_remote_copy(
-            src.at[:, :, pl.ds(pl.multiple_of(own + top, HALO), HALO), :],
-            src.at[:, :, pl.ds(there, HALO), :],
-            halo_send.at[2], halo_recv.at[2], device_id=across, device_id_type=MESH,
-        ),
-        pltpu.make_async_remote_copy(
-            ce.at[block, pl.ds(pl.multiple_of(own + top, HALO), HALO), :],
-            ce.at[block, pl.ds(there, HALO), :],
-            halo_send.at[3], halo_recv.at[3], device_id=across, device_id_type=MESH,
-        ),
-    ]
-    halos[0].start()
-    halos[1].start()
+    signal(near, near_peers)
+
+    def halo(n, source, target):
+        return pltpu.make_async_remote_copy(
+            source, target, halo_send.at[n], halo_recv.at[n],
+            device_id=across, device_id_type=MESH,
+        )
 
     own_slice = pl.ds(own, own_rows)
     halo_slice = pl.ds(pl.multiple_of(own + top, HALO), HALO)
     there_slice = pl.ds(there, HALO)
+    e_halos = [
+        halo(s, e_in.at[s, :, :, pl.ds(top, HALO), :], we.at[s, :, block, there_slice, :])
+        for s in range(2)
+    ]
+    h_halos = [
+        halo(
+            2 + s, h_in.at[s, :, :, pl.ds(top, HALO), :],
+            wh.at[s, :, block, pl.ds(there + HALO, HALO), :],
+        )
+        for s in range(2)
+    ]
+    src_halo = halo(4, src.at[:, :, halo_slice, :], src.at[:, :, there_slice, :])
+    ce_halo = halo(5, ce.at[block, halo_slice, :], ce.at[block, there_slice, :])
+    for s in range(2):
+        e_halos[s].start()
+        h_halos[s].start()
+
     high, low = pl.ds(X0 + width - 2, 2), pl.ds(X0, 2)
     high_ghost, low_ghost = pl.ds(X0 + width, 2), pl.ds(X0 - 2, 2)
 
@@ -201,7 +204,7 @@
         inv_eps = 1.0 / (1.0 + contrast * den[x] * flags)
         ce[X0 + x, own_slice, :] = inv_eps * gain1
         grad[x] = flags * contrast * inv_eps * inv_eps * step_dt
-    halos[3].start()
+    ce_halo.start()
     each(has_right, lambda: start_all(go_right))
     each(has_left, lambda: start_all(go_left))
     eye = lax.broadcasted_iota(jnp.int32, (own_rows, own_rows), 0) == lax.broadcasted_iota(
@@ -216,33 +219,21 @@
             column = jnp.sum(jnp.where(eye, row, 0.0), axis=1, keepdims=True)
             src[s, x, pl.ds(own, own_rows), :] = column * spot
 
-    halos[2].start()
-    signal(near, near_peers)
-    loads[2].wait()
-    loads[3].wait()
+    src_halo.start()
     loads[5].wait()
-    for halo in halos:
-        halo.wait()
-
-    def to_right(s, w, k):
-        return pltpu.make_async_remote_copy(
-            send_h.at[s, w, k], recv_h.at[s, w, k],
-            right_send.at[s, w, k], right_recv.at[s, w, k], device_id=right, device_id_type=MESH,
-        )
-
-    def to_left(s, w, k):
-        return pltpu.make_async_remote_copy(
-            send_e.at[s, w, k], recv_e.at[s, w, k],
-            left_send.at[s, w, k], left_recv.at[s, w, k], device_id=left, device_id_type=MESH,
-        )
+    loads[7].wait()
+    loads[8].wait()
+    def spread(row, n):
+        return jnp.broadcast_to(row, (n, depth))
 
     def up_z(f):
-        return jnp.where(last_lane, 0.0, pltpu.roll(f, depth - 1, 1))
+        return jnp.where(spread(lanes == depth - 1, f.shape[0]), 0.0, pltpu.roll(f, depth - 1, 1))
 
     def down_z(f):
-        return jnp.where(first_lane, 0.0, pltpu.roll(f, 1, 1))
+        return jnp.where(spread(lanes == 0, f.shape[0]), 0.0, pltpu.roll(f, 1, 1))
 
     def h_update(h_old, e, e_y, e_x, comps=(0, 1, 2)):
+        decay, gain, gain_half = (spread(r, e[0].shape[0]) for r in (decay1, gain1, gain_half1))
         new = {}
         if 0 in comps:
             new[0] = decay * h_old(0) - gain_half * ((e_y(2) - e[2]) - (up_z(e[1]) - e[1]))
@@ -251,6 +242,7 @@
         return new
 
     def e_update(e_old, h, h_y, h_x, c, drive):
+        decay = spread(decay1, h[0].shape[0])
         cx = c * inv_spacing
         x = decay * e_old(0) + cx * ((h[2] - h_y(2)) - (h[1] - down_z(h[1])))
         if drive is not None:
@@ -259,61 +251,123 @@
         z = decay * e_old(2) + (c * (h[1] - h_x[1]) - cx * (h[0] - h_y(0)))
         return {0: x, 1: y, 2: z}
 
-    R0, R1 = slice(0, rows), slice(1, rows + 1)
-    H0, HM = slice(HALO, HALO + rows), slice(HALO - 1, HALO + rows - 1)
-
-    def free(s, w):
-        for c in (1, 2):
-            send_e[s, w, 0, c - 1] = we[s, c, X0, R0, :]
-        each(has_left, lambda: to_left(s, w, 0).start())
+    def run_free(first, rest, put_left, put_right, material_of, drive_of):
+        put_left(0, first.e(1, 0, 0), first.e(2, 0, 0))
         for k in range(WIN):
             last = k == WIN - 1
+            now = first if k == 0 else rest
             h_planes = [x for x in range(width) if x >= k or x < width - 1 - k]
             if last:
                 h_planes = [width - 1]
             for x in h_planes:
-                if k == 0:
-                    old_h = lambda c, x=x: wh[s, c, X0 + x, H0, :]
-                    get_e = lambda c, x, r: we[s, c, X0 + x, r, :]
-                else:
-                    old_h = lambda c, x=x: fh[c, x + 1, H0, :]
-                    get_e = lambda c, x, r: fe[c, x, r, :]
-                e = {c: get_e(c, x, R0) for c in range(3)}
+                e = {c: now.e(c, x, 0) for c in range(3)}
                 e_x = {
-                    c: (get_e(c, x + 1, R0) if x < width - 1 else jnp.zeros_like(e[c]))
+                    c: (now.e(c, x + 1, 0) if x < width - 1 else jnp.zeros_like(e[c]))
                     for c in (1, 2)
                 }
                 new = h_update(
-                    old_h, e, lambda c, x=x: get_e(c, x, R1), e_x, (1, 2) if last else (0, 1, 2)
+                    lambda c: now.h(c, x, 0), e, lambda c: now.e(c, x, 1), e_x,
+                    (1, 2) if last else (0, 1, 2),
                 )
                 if not last:
                     for c in range(3):
-                        fh[c, x + 1, H0, :] = new[c]
+                        rest.set_h(c, x, new[c])
                 if x == width - 1:
-                    send_h[s, w, k, 0] = new[1]
-                    send_h[s, w, k, 1] = new[2]
-            each(has_right, lambda: to_right(s, w, k).start())
+                    edge = new
+            put_right(k, edge[1], edge[2])
             if last:
                 break
-            wave = waves[s, w * WIN + k]
-            e_planes = [x for x in range(width) if x >= k + 1 or x < width - 1 - k]
-            for x in e_planes:
-                if k == 0:
-                    old_e = lambda c, x=x: we[s, c, X0 + x, R0, :]
-                else:
-                    old_e = lambda c, x=x: fe[c, x, R0, :]
-                h = {c: fh[c, x + 1, H0, :] for c in range(3)}
-                h_x = {c: fh[c, x, H0, :] for c in (1, 2)}
+            for x in [x for x in range(width) if x >= k + 1 or x < width - 1 - k]:
+                h = {c: rest.h(c, x, 0) for c in range(3)}
+                h_x = {c: rest.h(c, x - 1, 0) for c in (1, 2)}
                 new = e_update(
-                    old_e, h, lambda c, x=x: fh[c, x + 1, HM, :], h_x,
-                    ce[X0 + x], src[s, x] * wave,
+                    lambda c: now.e(c, x, 0), h, lambda c: rest.h(c, x, -1), h_x,
+                    material_of(x), drive_of(x, k),
                 )
                 for c in range(3):
-                    fe[c, x, R0, :] = new[c]
+                    rest.set_e(c, x, new[c])
                 if x == 0:
-                    send_e[s, w, k + 1, 0] = new[1]
-                    send_e[s, w, k + 1, 1] = new[2]
-            each(has_left, lambda: to_left(s, w, k + 1).start())
+                    edge = new
+            put_left(k + 1, edge[1], edge[2])
+
+    class Fields:
+        def __init__(self, e_ref, h_ref, e_x, h_x, e_row, h_row, n):
+            self.e_ref, self.h_ref, self.e_x, self.h_x = e_ref, h_ref, e_x, h_x
+            self.e_row, self.h_row, self.n = e_row, h_row, n
+
+        def e(self, c, x, dy):
+            return self.e_ref[c, self.e_x + x, self.e_row + dy : self.e_row + dy + self.n, :]
+
+        def h(self, c, x, dy):
+            return self.h_ref[c, self.h_x + x, self.h_row + dy : self.h_row + dy + self.n, :]
+
+        def set_e(self, c, x, value):
+            self.e_ref[c, self.e_x + x, self.e_row : self.e_row + self.n, :] = value
+
+        def set_h(self, c, x, value):
+            self.h_ref[c, self.h_x + x, self.h_row : self.h_row + self.n, :] = value
+
+    def to_side(go_right, s, w, k, spare=None, part=None):
+        source, target = (send_h, recv_h) if go_right else (send_e, recv_e)
+        source, target = source.at[s, w if spare is None else spare, k], target.at[s, w, k]
+        if part is not None:
+            source, target = source.at[:, part], target.at[:, part]
+        send, recv = (right_send, right_recv) if go_right else (left_send, left_recv)
+        return pltpu.make_async_remote_copy(
+            source, target, send.at[s, w, k], recv.at[s, w, k],
+            device_id=right if go_right else left, device_id_type=MESH,
+        )
+
+    far_rows = pl.ds(pl.multiple_of(gy * 2 * HALO, HALO), own_rows - HALO)
+    near_rows = pl.ds(pl.multiple_of((1 - gy) * (own_rows - HALO), HALO), 2 * HALO)
+
+    def early():
+        fields = Fields(pe, ph, 0, 1, HALO, HALO, own_rows)
+
+        def put(go_right, k, y, z):
+            buffer = send_h if go_right else send_e
+            buffer[0, WINDOWS, k, 0, own_slice, :] = y
+            buffer[0, WINDOWS, k, 1, own_slice, :] = z
+            each(
+                has_right if go_right else has_left,
+                lambda: to_side(go_right, 0, 0, k, WINDOWS, far_rows).start(),
+            )
+
+        run_free(
+            fields, fields,
+            lambda k, y, z: put(False, k, y, z), lambda k, y, z: put(True, k, y, z),
+            lambda x: ce[X0 + x, own_slice, :],
+            lambda x, k: src[0, x, own_slice, :] * waves[0, k],
+        )
+
+    def free(s, w):
+        def put(go_right, k, y, z):
+            buffer = send_h if go_right else send_e
+            buffer[s, w, k, 0] = y
+            buffer[s, w, k, 1] = z
+            there_is = has_right if go_right else has_left
+            if w == 0:
+                each(
+                    jnp.logical_and(there_is, s == 0),
+                    lambda: to_side(go_right, s, w, k, None, near_rows).start(),
+                )
+                each(
+                    jnp.logical_and(there_is, s != 0),
+                    lambda: to_side(go_right, s, w, k).start(),
+                )
+            else:
+                each(there_is, lambda: to_side(go_right, s, w, k).start())
+
+        run_free(
+            Fields(we.at[s], wh.at[s], X0, X0, 0, HALO, rows),
+            Fields(fe, fh, 0, 1, 0, HALO, rows),
+            lambda k, y, z: put(False, k, y, z), lambda k, y, z: put(True, k, y, z),
+            lambda x: ce[X0 + x],
+            lambda x, k: src[s, x] * waves[s, w * WIN + k],
+        )
+
+    H0, HM = slice(HALO, HALO + rows), slice(HALO - 1, HALO + rows - 1)
+    R0, R1 = slice(0, rows), slice(1, rows + 1)
 
     def true(s, w, relay):
         for c in range(3):
@@ -326,7 +380,7 @@
             e_out_reach = min(k + 1, WIN - 1 - k)
             if k == WIN - 2:
                 relay()
-            each(has_right, lambda: to_left(s, w, k).wait_recv())
+            each(has_right, lambda: to_side(False, s, w, k).wait_recv())
             e_next = None
             for x in range(h_hi - 1, h_lo - 1, -1):
                 p = X0 + x
@@ -343,7 +397,7 @@
                 )
                 for c in range(3):
                     wh[s, c, p, H0, :] = new[c]
-            each(has_left, lambda: to_right(s, w, k).wait_recv())
+            each(has_left, lambda: to_side(True, s, w, k).wait_recv())
             wave = waves[s, w * WIN + k]
             h_last = None
             for x in range(-e_out_reach, width + e_out_reach):
@@ -366,13 +420,26 @@
                     if inside:
                         hist[s, w * WIN + k, c, x] = new[c]
 
+    early()
+    loads[2].wait()
+    loads[3].wait()
+    src_halo.wait()
+    ce_halo.wait()
+    e_halos[0].wait()
+    h_halos[0].wait()
+
     def start_free(s, carry):
+        @pl.when(s == 1)
+        def _():
+            e_halos[1].wait()
+            h_halos[1].wait()
+
         free(s, 0)
         return carry
 
-    lax.fori_loop(0, 2, start_free, 0)
     pl.semaphore_wait(near, len(near_peers))
     signal(mid, mid_peers)
+    lax.fori_loop(0, 2, start_free, 0)
 
     def wait_recvs(copies):
         for copy in copies:
@@ -420,7 +487,7 @@
         def _():
             free(s, 1)
 
-        @pl.when(j == 1)
+        @pl.when(j == 0)
         def _():
             pl.semaphore_wait(mid, len(mid_peers))
             signal(far, far_peers)
@@ -452,6 +519,20 @@
                 )
         grad[x] = grad[x] * corr
 
+    each(has_right, lambda: wait_sends(go_right))
+    each(has_left, lambda: wait_sends(go_left))
+    for copy in sum1 + sum2:
+        copy.wait_send()
+
+    def drain(j, carry):
+        w, s = j // 2, lax.rem(j, 2)
+        for k in range(WIN):
+            each(has_right, lambda: to_side(True, s, w, k).wait_send())
+            each(has_left, lambda: to_side(False, s, w, k).wait_send())
+        return carry
+
+    lax.fori_loop(0, 2 * WINDOWS, drain, 0)
+
     for copy in sum2:
         copy.wait_recv()
     total = part2[0]
@@ -462,19 +543,6 @@
     scale = jnp.broadcast_to(1.0 / (power + small_eps), (own_rows, depth))
     for x in range(width):
         grad[x] = grad[x] * scale
-    each(has_right, lambda: wait_sends(go_right))
-    each(has_left, lambda: wait_sends(go_left))
-    for copy in sum1 + sum2:
-        copy.wait_send()
-
-    def drain(j, carry):
-        w, s = j // 2, lax.rem(j, 2)
-        for k in range(WIN):
-            each(has_right, lambda: to_right(s, w, k).wait_send())
-            each(has_left, lambda: to_left(s, w, k).wait_send())
-        return carry
-
-    lax.fori_loop(0, 2 * WINDOWS, drain, 0)
 
 
 def store(we, wh, grad, e_out, h_out, g_out, sem):
@@ -506,7 +574,8 @@
     count_z = lax.axis_size("gx") // CHIPS_X
     f32 = jnp.float32
     vmem, dma = pltpu.VMEM, pltpu.SemaphoreType.DMA
-    series = vmem((sets, WINDOWS, WIN, 2, rows, depth), f32)
+    came = vmem((sets, WINDOWS, WIN, 2, rows, depth), f32)
+    sent = vmem((sets, WINDOWS + 1, WIN, 2, rows, depth), f32)
     any_space = pl.BlockSpec(memory_space=pl.ANY)
     held = pl.BlockSpec(memory_space=pltpu.VMEM)
     smem, wait = pltpu.SMEM, pltpu.SemaphoreType.REGULAR
@@ -517,9 +586,8 @@
         in_specs=[any_space] * 7,
         out_specs=(held,) * 3,
         scratch_shapes=[
-            vmem((comps, width + 1, rows + HALO, depth), f32),
-            vmem((comps, width + 1, rows + HALO, depth), f32),
-            series, series, series, series,
+            *[vmem((comps, width + 1, rows + HALO, depth), f32)] * 4,
+            sent, sent, came, came,
             vmem((FRAME, rows, depth), f32),
             vmem((sets, width, rows, depth), f32),
             vmem((width, own_rows, depth), f32),
@@ -530,7 +598,7 @@
             smem(planes.shape, jnp.int32),
             smem(waveforms.shape, f32),
             vmem(profiles.shape, f32),
-            dma((7,)), wait, wait, wait, dma((4,)), dma((4,)), dma((4,)), dma((4,)),
+            dma((9,)), wait, wait, wait, dma((6,)), dma((6,)), dma((4,)), dma((4,)),
             dma((sets, WINDOWS, WIN)), dma((sets, WINDOWS, WIN)),
             dma((sets, WINDOWS, WIN)), dma((sets, WINDOWS, WIN)),
             dma((2 * CHIPS_X - 1,)), dma((2 * CHIPS_X - 1,)),

time: 52.8 us -> 49.9 us (0.945)
  Pallas kernels: 52.1 us -> 49.2 us
    pallas_call x1, Pallas kernels: 51.1 us -> 48.2 us  [shards(): pl.pallas_call(kernel, out_shape=(vmem_array(frame), vmem_array(frame), v...]
where the time goes in v4:
time: 49.9 us; the launch traced here: 49.8 us
  Pallas kernels  49.2 us (99%)
  between operations  0.64 us (1%)
    pallas_call x1, Pallas kernels, shards(): pl.pallas_call(kernel, out_shape=(vmem_array(frame), vmem_array(frame), v...  48.2 us

profile of v4, /device:TPU:40, one launch (start us, length us, event | category | flops | bytes accessed | tf_op | source)
XLA Modules:
  0.0 49.8 jit_solution(5732119241103590940)
XLA Ops:
  0.6 48.2 %shard_map.94 = (f32[2,3,9,48,128]{4,3,2,1,0:T(8,128)S(1)}, f32[2,3,9,48,128]{4,3,2,1,0:T(8,128)S(1)}, f32[4,32,128]{2,1,0:T(8,128)S(1)}) custom-call(s32[2]{0:T(128)} %planes_in.1, f32[2,8]{1,0:T(2,128)} %waves_in.1, f32[2,4,32]{2,1,0:T(4,128)} %prof_in.1, f32[2,3,4,32,128]{4,3,2,1,0:T(8,128)} %e_in.1, f32[2,3,4,32,128]{4,3,2,1,0:T(8,128)} %h_in.1, ...), custom_call_target="tpu_custom_call" | custom-call | tf_op jit(solution)/shard_map/pallas_call | solution.py:583
  48.9 0.9 %shard_map.95 = (f32[2,3,4,32,128]{4,3,2,1,0:T(8,128)}, f32[2,3,4,32,128]{4,3,2,1,0:T(8,128)}, f32[4,32,128]{2,1,0:T(8,128)}) custom-call(f32[2,3,9,48,128]{4,3,2,1,0:T(8,128)S(1)} %get-tuple-element.6.we, f32[2,3,9,48,128]{4,3,2,1,0:T(8,128)S(1)} %get-tuple-element.7.wh, f32[4,32,128]{2,1,0:T(8,128)S(1)} %get-tuple-element.8.grad), custom_call_target="tpu_custom_call" | custom-call | tf_op jit(solution)/shard_map/pallas_call | solution.py:611

commit v5 on v4

--- a/solution.py
+++ b/solution.py
@@ -318,8 +318,19 @@
             device_id=right if go_right else left, device_id_type=MESH,
         )
 
+    def depth_of(go_right, w, k):
+        return STEPS - (w * WIN + k) - (1 if go_right else 0)
+
+    def used_rows(go_right, w, k):
+        extra = depth_of(go_right, w, k)
+        return pl.ds(gy * (HALO - extra), own_rows + extra)
+
     far_rows = pl.ds(pl.multiple_of(gy * 2 * HALO, HALO), own_rows - HALO)
-    near_rows = pl.ds(pl.multiple_of((1 - gy) * (own_rows - HALO), HALO), 2 * HALO)
+
+    def near_rows(go_right, w, k):
+        extra = depth_of(go_right, w, k)
+        start = own_rows - HALO
+        return pl.ds(start - gy * (start - HALO + extra), HALO + extra)
 
     def early():
         fields = Fields(pe, ph, 0, 1, HALO, HALO, own_rows)
@@ -346,17 +357,19 @@
             buffer[s, w, k, 0] = y
             buffer[s, w, k, 1] = z
             there_is = has_right if go_right else has_left
+            whole = used_rows(go_right, w, k)
             if w == 0:
+                parted = (s == 0) & (gy == 0)
                 each(
-                    jnp.logical_and(there_is, s == 0),
-                    lambda: to_side(go_right, s, w, k, None, near_rows).start(),
+                    there_is & parted,
+                    lambda: to_side(go_right, s, w, k, None, near_rows(go_right, w, k)).start(),
                 )
                 each(
-                    jnp.logical_and(there_is, s != 0),
-                    lambda: to_side(go_right, s, w, k).start(),
+                    there_is & jnp.logical_not(parted),
+                    lambda: to_side(go_right, s, w, k, None, whole).start(),
                 )
             else:
-                each(there_is, lambda: to_side(go_right, s, w, k).start())
+                each(there_is, lambda: to_side(go_right, s, w, k, None, whole).start())
 
         run_free(
             Fields(we.at[s], wh.at[s], X0, X0, 0, HALO, rows),
@@ -368,6 +381,14 @@
 
     H0, HM = slice(HALO, HALO + rows), slice(HALO - 1, HALO + rows - 1)
     R0, R1 = slice(0, rows), slice(1, rows + 1)
+
+    def wait_series(there_is, go_right, s, w, k):
+        for window in range(WINDOWS):
+            rows_in = used_rows(go_right, window, k)
+            each(
+                there_is & (w == window),
+                lambda: to_side(go_right, s, window, k, None, rows_in).wait_recv(),
+            )
 
     def true(s, w, relay):
         for c in range(3):
@@ -380,7 +401,7 @@
             e_out_reach = min(k + 1, WIN - 1 - k)
             if k == WIN - 2:
                 relay()
-            each(has_right, lambda: to_side(False, s, w, k).wait_recv())
+            wait_series(has_right, False, s, w, k)
             e_next = None
             for x in range(h_hi - 1, h_lo - 1, -1):
                 p = X0 + x
@@ -397,7 +418,7 @@
                 )
                 for c in range(3):
                     wh[s, c, p, H0, :] = new[c]
-            each(has_left, lambda: to_side(True, s, w, k).wait_recv())
+            wait_series(has_left, True, s, w, k)
             wave = waves[s, w * WIN + k]
             h_last = None
             for x in range(-e_out_reach, width + e_out_reach):
@@ -420,7 +441,7 @@
                     if inside:
                         hist[s, w * WIN + k, c, x] = new[c]
 
-    early()
+    pl.when(gy == 0)(early)
     loads[2].wait()
     loads[3].wait()
     src_halo.wait()
@@ -524,14 +545,15 @@
     for copy in sum1 + sum2:
         copy.wait_send()
 
-    def drain(j, carry):
-        w, s = j // 2, lax.rem(j, 2)
-        for k in range(WIN):
-            each(has_right, lambda: to_side(True, s, w, k).wait_send())
-            each(has_left, lambda: to_side(False, s, w, k).wait_send())
+    def drain(s, carry):
+        for w in range(WINDOWS):
+            for k in range(WIN):
+                for go_right, there_is in ((True, has_right), (False, has_left)):
+                    copy = to_side(go_right, s, w, k, None, used_rows(go_right, w, k))
+                    each(there_is, copy.wait_send)
         return carry
 
-    lax.fori_loop(0, 2 * WINDOWS, drain, 0)
+    lax.fori_loop(0, 2, drain, 0)
 
     for copy in sum2:
         copy.wait_recv()

time: 49.9 us -> 48.6 us (0.974)
  Pallas kernels: 49.2 us -> 47.8 us
    pallas_call x1, Pallas kernels: 48.2 us -> 46.9 us  [shards(): pl.pallas_call(kernel, out_shape=(vmem_array(frame), vmem_array(frame), v...]
where the time goes in v5:
time: 48.6 us; the launch traced here: 48.5 us
  Pallas kernels  47.8 us (98%)
  between operations  0.64 us (1%)
    pallas_call x1, Pallas kernels, shards(): pl.pallas_call(kernel, out_shape=(vmem_array(frame), vmem_array(frame), v...  46.9 us

profile of v5, /device:TPU:40, one launch (start us, length us, event | category | flops | bytes accessed | tf_op | source)
XLA Modules:
  0.0 48.5 jit_solution(2409385141295642194)
XLA Ops:
  0.6 46.9 %shard_map.94 = (f32[2,3,9,48,128]{4,3,2,1,0:T(8,128)S(1)}, f32[2,3,9,48,128]{4,3,2,1,0:T(8,128)S(1)}, f32[4,32,128]{2,1,0:T(8,128)S(1)}) custom-call(s32[2]{0:T(128)} %planes_in.1, f32[2,8]{1,0:T(2,128)} %waves_in.1, f32[2,4,32]{2,1,0:T(4,128)} %prof_in.1, f32[2,3,4,32,128]{4,3,2,1,0:T(8,128)} %e_in.1, f32[2,3,4,32,128]{4,3,2,1,0:T(8,128)} %h_in.1, ...), custom_call_target="tpu_custom_call" | custom-call | tf_op jit(solution)/shard_map/pallas_call | solution.py:605
  47.5 0.9 %shard_map.95 = (f32[2,3,4,32,128]{4,3,2,1,0:T(8,128)}, f32[2,3,4,32,128]{4,3,2,1,0:T(8,128)}, f32[4,32,128]{2,1,0:T(8,128)}) custom-call(f32[2,3,9,48,128]{4,3,2,1,0:T(8,128)S(1)} %get-tuple-element.6.we, f32[2,3,9,48,128]{4,3,2,1,0:T(8,128)S(1)} %get-tuple-element.7.wh, f32[4,32,128]{2,1,0:T(8,128)S(1)} %get-tuple-element.8.grad), custom_call_target="tpu_custom_call" | custom-call | tf_op jit(solution)/shard_map/pallas_call | solution.py:633

commit v6 on v5

--- a/solution.py
+++ b/solution.py
@@ -45,7 +45,7 @@
     right_across, left_across = dict(right, gy=other), dict(left, gy=other)
     has_right, has_left = gx < count_x - 1, gx > 0
     plane_peers = []
-    for dx in range(CHIPS_X):
+    for dx in sorted(range(CHIPS_X), key=lambda d: -min(d, CHIPS_X - d)):
         for dc in range(2):
             if dx or dc:
                 peer = lax.rem(chip_x + dx, CHIPS_X) * count_z + chip_z
@@ -83,8 +83,8 @@
         pltpu.make_async_copy(e_in.at[0], pe.at[:, pl.ds(0, width), early_rows], load_sem.at[7]),
         pltpu.make_async_copy(h_in.at[0], ph.at[:, pl.ds(1, width), early_rows], load_sem.at[8]),
     ]
-    for load in loads:
-        load.start()
+    for n in (0, 1, 4, 6, 7, 8, 5, 2, 3):
+        loads[n].start()
 
     def signal(semaphore, peers):
         for peer in peers:
@@ -142,7 +142,6 @@
             ce[p] = plane0
 
     pl.semaphore_wait(barrier, len(peers))
-    signal(near, near_peers)
 
     def halo(n, source, target):
         return pltpu.make_async_remote_copy(
@@ -169,6 +168,7 @@
     for s in range(2):
         e_halos[s].start()
         h_halos[s].start()
+    signal(near, near_peers)
 
     high, low = pl.ds(X0 + width - 2, 2), pl.ds(X0, 2)
     high_ghost, low_ghost = pl.ds(X0 + width, 2), pl.ds(X0 - 2, 2)

time: 48.6 us -> 48.6 us (level)
  no operation moved by 1% of the time
where the time goes in v6:
time: 48.6 us; the launch traced here: 48.5 us
  Pallas kernels  47.8 us (98%)
  between operations  0.64 us (1%)
    pallas_call x1, Pallas kernels, shards(): pl.pallas_call(kernel, out_shape=(vmem_array(frame), vmem_array(frame), v...  46.9 us

profile of v6, /device:TPU:40, one launch (start us, length us, event | category | flops | bytes accessed | tf_op | source)
XLA Modules:
  0.0 48.5 jit_solution(13208888473064504013)
XLA Ops:
  0.6 46.9 %shard_map.94 = (f32[2,3,9,48,128]{4,3,2,1,0:T(8,128)S(1)}, f32[2,3,9,48,128]{4,3,2,1,0:T(8,128)S(1)}, f32[4,32,128]{2,1,0:T(8,128)S(1)}) custom-call(s32[2]{0:T(128)} %planes_in.1, f32[2,8]{1,0:T(2,128)} %waves_in.1, f32[2,4,32]{2,1,0:T(4,128)} %prof_in.1, f32[2,3,4,32,128]{4,3,2,1,0:T(8,128)} %e_in.1, f32[2,3,4,32,128]{4,3,2,1,0:T(8,128)} %h_in.1, ...), custom_call_target="tpu_custom_call" | custom-call | tf_op jit(solution)/shard_map/pallas_call | solution.py:605
  47.5 0.9 %shard_map.95 = (f32[2,3,4,32,128]{4,3,2,1,0:T(8,128)}, f32[2,3,4,32,128]{4,3,2,1,0:T(8,128)}, f32[4,32,128]{2,1,0:T(8,128)}) custom-call(f32[2,3,9,48,128]{4,3,2,1,0:T(8,128)S(1)} %get-tuple-element.6.we, f32[2,3,9,48,128]{4,3,2,1,0:T(8,128)S(1)} %get-tuple-element.7.wh, f32[4,32,128]{2,1,0:T(8,128)S(1)} %get-tuple-element.8.grad), custom_call_target="tpu_custom_call" | custom-call | tf_op jit(solution)/shard_map/pallas_call | solution.py:633

commit v7 on v6

--- a/solution.py
+++ b/solution.py
@@ -205,8 +205,8 @@
         ce[X0 + x, own_slice, :] = inv_eps * gain1
         grad[x] = flags * contrast * inv_eps * inv_eps * step_dt
     ce_halo.start()
-    each(has_right, lambda: start_all(go_right))
-    each(has_left, lambda: start_all(go_left))
+    each(has_right & (gy == 0), lambda: start_all(go_right))
+    each(has_left & (gy == 0), lambda: start_all(go_left))
     eye = lax.broadcasted_iota(jnp.int32, (own_rows, own_rows), 0) == lax.broadcasted_iota(
         jnp.int32, (own_rows, own_rows), 1
     )
@@ -442,6 +442,8 @@
                         hist[s, w * WIN + k, c, x] = new[c]
 
     pl.when(gy == 0)(early)
+    each(has_right & (gy != 0), lambda: start_all(go_right))
+    each(has_left & (gy != 0), lambda: start_all(go_left))
     loads[2].wait()
     loads[3].wait()
     src_halo.wait()
@@ -571,11 +573,18 @@
     width, own_rows = grad.shape[0], grad.shape[1]
     own = pl.multiple_of(lax.axis_index("gy") * HALO, HALO)
     block = pl.ds(LEFT, width)
-    outs = [
-        pltpu.make_async_copy(we.at[:, :, block, pl.ds(own, own_rows), :], e_out, sem.at[0]),
-        pltpu.make_async_copy(wh.at[:, :, block, pl.ds(own + HALO, own_rows), :], h_out, sem.at[1]),
-        pltpu.make_async_copy(grad, g_out, sem.at[2]),
-    ]
+    outs = [pltpu.make_async_copy(grad, g_out, sem.at[0])]
+    for s in range(we.shape[0]):
+        outs.append(
+            pltpu.make_async_copy(
+                we.at[s, :, block, pl.ds(own, own_rows), :], e_out.at[s], sem.at[1 + s]
+            )
+        )
+        outs.append(
+            pltpu.make_async_copy(
+                wh.at[s, :, block, pl.ds(own + HALO, own_rows), :], h_out.at[s], sem.at[3 + s]
+            )
+        )
     for out in outs:
         out.start()
     for out in outs:
@@ -639,7 +648,7 @@
         ),
         in_specs=[held] * 3,
         out_specs=(any_space,) * 3,
-        scratch_shapes=[dma((3,))],
+        scratch_shapes=[dma((5,))],
         compiler_params=pltpu.CompilerParams(vmem_limit_bytes=4 << 20),
     )(in_vmem(e_frame), in_vmem(h_frame), in_vmem(grad))
 

time: 48.6 us -> 48.6 us (level)
  no operation moved by 1% of the time
where the time goes in v7:
time: 48.6 us; the launch traced here: 48.5 us
  Pallas kernels  47.8 us (98%)
  between operations  0.64 us (1%)
    pallas_call x1, Pallas kernels, shards(): pl.pallas_call(kernel, out_shape=(vmem_array(frame), vmem_array(frame), v...  46.9 us

profile of v7, /device:TPU:40, one launch (start us, length us, event | category | flops | bytes accessed | tf_op | source)
XLA Modules:
  0.0 48.5 jit_solution(1271304477751509207)
XLA Ops:
  0.6 46.9 %shard_map.94 = (f32[2,3,9,48,128]{4,3,2,1,0:T(8,128)S(1)}, f32[2,3,9,48,128]{4,3,2,1,0:T(8,128)S(1)}, f32[4,32,128]{2,1,0:T(8,128)S(1)}) custom-call(s32[2]{0:T(128)} %planes_in.1, f32[2,8]{1,0:T(2,128)} %waves_in.1, f32[2,4,32]{2,1,0:T(4,128)} %prof_in.1, f32[2,3,4,32,128]{4,3,2,1,0:T(8,128)} %e_in.1, f32[2,3,4,32,128]{4,3,2,1,0:T(8,128)} %h_in.1, ...), custom_call_target="tpu_custom_call" | custom-call | tf_op jit(solution)/shard_map/pallas_call | solution.py:614
  47.5 0.9 %shard_map.95 = (f32[2,3,4,32,128]{4,3,2,1,0:T(8,128)}, f32[2,3,4,32,128]{4,3,2,1,0:T(8,128)}, f32[4,32,128]{2,1,0:T(8,128)}) custom-call(f32[2,3,9,48,128]{4,3,2,1,0:T(8,128)S(1)} %get-tuple-element.6.we, f32[2,3,9,48,128]{4,3,2,1,0:T(8,128)S(1)} %get-tuple-element.7.wh, f32[4,32,128]{2,1,0:T(8,128)S(1)} %get-tuple-element.8.grad), custom_call_target="tpu_custom_call" | custom-call | tf_op jit(solution)/shard_map/pallas_call | solution.py:642

commit v8 on v7

--- a/solution.py
+++ b/solution.py
@@ -45,7 +45,7 @@
     right_across, left_across = dict(right, gy=other), dict(left, gy=other)
     has_right, has_left = gx < count_x - 1, gx > 0
     plane_peers = []
-    for dx in sorted(range(CHIPS_X), key=lambda d: -min(d, CHIPS_X - d)):
+    for dx in range(CHIPS_X):
         for dc in range(2):
             if dx or dc:
                 peer = lax.rem(chip_x + dx, CHIPS_X) * count_z + chip_z
@@ -83,8 +83,8 @@
         pltpu.make_async_copy(e_in.at[0], pe.at[:, pl.ds(0, width), early_rows], load_sem.at[7]),
         pltpu.make_async_copy(h_in.at[0], ph.at[:, pl.ds(1, width), early_rows], load_sem.at[8]),
     ]
-    for n in (0, 1, 4, 6, 7, 8, 5, 2, 3):
-        loads[n].start()
+    for load in loads:
+        load.start()
 
     def signal(semaphore, peers):
         for peer in peers:
@@ -142,6 +142,7 @@
             ce[p] = plane0
 
     pl.semaphore_wait(barrier, len(peers))
+    signal(near, near_peers)
 
     def halo(n, source, target):
         return pltpu.make_async_remote_copy(
@@ -168,7 +169,6 @@
     for s in range(2):
         e_halos[s].start()
         h_halos[s].start()
-    signal(near, near_peers)
 
     high, low = pl.ds(X0 + width - 2, 2), pl.ds(X0, 2)
     high_ghost, low_ghost = pl.ds(X0 + width, 2), pl.ds(X0 - 2, 2)
@@ -205,8 +205,8 @@
         ce[X0 + x, own_slice, :] = inv_eps * gain1
         grad[x] = flags * contrast * inv_eps * inv_eps * step_dt
     ce_halo.start()
-    each(has_right & (gy == 0), lambda: start_all(go_right))
-    each(has_left & (gy == 0), lambda: start_all(go_left))
+    each(has_right, lambda: start_all(go_right))
+    each(has_left, lambda: start_all(go_left))
     eye = lax.broadcasted_iota(jnp.int32, (own_rows, own_rows), 0) == lax.broadcasted_iota(
         jnp.int32, (own_rows, own_rows), 1
     )
@@ -442,8 +442,6 @@
                         hist[s, w * WIN + k, c, x] = new[c]
 
     pl.when(gy == 0)(early)
-    each(has_right & (gy != 0), lambda: start_all(go_right))
-    each(has_left & (gy != 0), lambda: start_all(go_left))
     loads[2].wait()
     loads[3].wait()
     src_halo.wait()

time: 48.6 us -> 48.6 us (level)
  no operation moved by 1% of the time
where the time goes in v8:
time: 48.6 us; the launch traced here: 48.5 us
  Pallas kernels  47.8 us (98%)
  between operations  0.64 us (1%)
    pallas_call x1, Pallas kernels, shards(): pl.pallas_call(kernel, out_shape=(vmem_array(frame), vmem_array(frame), v...  46.9 us

profile of v8, /device:TPU:40, one launch (start us, length us, event | category | flops | bytes accessed | tf_op | source)
XLA Modules:
  0.0 48.5 jit_solution(15785008502872138180)
XLA Ops:
  0.6 46.9 %shard_map.94 = (f32[2,3,9,48,128]{4,3,2,1,0:T(8,128)S(1)}, f32[2,3,9,48,128]{4,3,2,1,0:T(8,128)S(1)}, f32[4,32,128]{2,1,0:T(8,128)S(1)}) custom-call(s32[2]{0:T(128)} %planes_in.1, f32[2,8]{1,0:T(2,128)} %waves_in.1, f32[2,4,32]{2,1,0:T(4,128)} %prof_in.1, f32[2,3,4,32,128]{4,3,2,1,0:T(8,128)} %e_in.1, f32[2,3,4,32,128]{4,3,2,1,0:T(8,128)} %h_in.1, ...), custom_call_target="tpu_custom_call" | custom-call | tf_op jit(solution)/shard_map/pallas_call | solution.py:612
  47.5 0.9 %shard_map.95 = (f32[2,3,4,32,128]{4,3,2,1,0:T(8,128)}, f32[2,3,4,32,128]{4,3,2,1,0:T(8,128)}, f32[4,32,128]{2,1,0:T(8,128)}) custom-call(f32[2,3,9,48,128]{4,3,2,1,0:T(8,128)S(1)} %get-tuple-element.6.we, f32[2,3,9,48,128]{4,3,2,1,0:T(8,128)S(1)} %get-tuple-element.7.wh, f32[4,32,128]{2,1,0:T(8,128)S(1)} %get-tuple-element.8.grad), custom_call_target="tpu_custom_call" | custom-call | tf_op jit(solution)/shard_map/pallas_call | solution.py:640
